TPU v7x, 128 devices: a whole 4x4x4 slice. The times are simulated.
128 devices in a mesh: dp: 4 (over y), ctx: 32 (over x, z, core).
Axes of the slice: x: 4, y: 4, z: 4, core: 2. Of those that a mesh axis runs over, the one named last changes fastest.
Arguments:
- tokens: bfloat16 [32768, 1024], P(('dp', 'ctx')), parts along dimension 0, may hold values from -48 to 48
- w_query: bfloat16 [1024, 1024], replicated
- w_key: bfloat16 [1024, 1024], replicated
- w_value: bfloat16 [1024, 1024], replicated, may hold values from -0.1875 to 0.1875
- w_out: bfloat16 [1024, 1024], replicated, may hold values from -0.5 to 0.5
- norm_gain: float32 [1024], replicated, may hold values from 0.5 to 1.5
- norm_bias: float32 [1024], replicated, may hold values from -4 to 4
- w_pool: bfloat16 [1024, 1024], replicated, may hold values from -0.1875 to 0.1875
- pool_bias: float32 [1024], replicated, may hold values from -6 to 6
- random_ids: int32 [512, 16, 3], P(('dp', 'ctx')), parts along dimension 0, may hold values from 0 to 127, as said below
- lengths: int32 [32], P('dp'), parts along dimension 0, may hold values from 1 to 2048, 8192 in all
Outputs:
- encoded: bfloat16 [32768, 1024], P(('dp', 'ctx')), parts along dimension 0
- doc_vectors: float32 [32, 1024], P('dp'), parts along dimension 0
There are 4 independent parts, one for each index of `dp`. A program takes and returns all parts, laid end to end along the dimension named above; an argument that names none is the same for every part. Nothing has to cross between parts.
Inputs may be any that keep to these rules, and one draw needn't show every extreme that they name: `random_ids`: entry [b, h, r] is the key block of the r-th random block of query block b and head h. Among the 192 entries of the rows of one device, at most 8 name blocks of the range i * 4 to (i + 1) * 4 - 1 of any one device i; in every draw some device's range is named by exactly 8 entries of the rows of every device.
All inputs are finite; a program needn't handle non-finite values.
Results may differ from a plain program's by a relative error of at most 0.0089.
Values may be sent and summed in bfloat16 or wider, within the bound.
A program may use at most 128 MiB of HBM per device.

v0:
```python
import jax
import jax.numpy as jnp
from jax import lax
from jax.sharding import PartitionSpec as P

HEADS = 16
BLK = 64
RAND = 3


masked_score = -30000.0


def with_halo(cells, sides, width):
    for axis, dim in sides:
        count = lax.axis_size(axis)
        ends = count - 1
        head = lax.slice_in_dim(cells, 0, width, axis=dim)
        tail = lax.slice_in_dim(cells, cells.shape[dim] - width, cells.shape[dim], axis=dim)
        cells = jnp.concatenate(
            [
                lax.ppermute(tail, axis, [(i, (i + 1) % count) for i in range(ends)]),
                cells,
                lax.ppermute(head, axis, [((i + 1) % count, i) for i in range(ends)]),
            ],
            axis=dim,
        )
    return cells


def doc_number(positions, doc_ends):
    return jnp.sum((positions[..., None] >= doc_ends).astype(jnp.int32), axis=-1)


def partial_attention(
    queries, keys_in, values_in, query_pos, key_pos, doc_ends, seq_total, by_document
):
    score_scale = queries.shape[-1] ** (-0.5)
    scores = (
        jnp.einsum("...qd,...kd->...qk", queries, keys_in, preferred_element_type=jnp.float32)
        * score_scale
    )
    inside = ((key_pos >= 0) & (key_pos < seq_total))[..., None, :]
    if by_document:
        same_doc = (
            doc_number(query_pos, doc_ends)[..., :, None]
            == doc_number(key_pos, doc_ends)[..., None, :]
        )
        inside = same_doc & inside
    scores = jnp.where(inside, scores, masked_score)
    row_max = jnp.max(scores, axis=-1)
    weights = jnp.exp(scores - row_max[..., None])
    row_total = jnp.sum(weights, axis=-1)
    partial_out = jnp.einsum(
        "...qk,...kd->...qd",
        weights.astype(jnp.bfloat16),
        values_in,
        preferred_element_type=jnp.float32,
    )
    return (row_max, row_total, partial_out)


def combine(win_parts, rand_parts):
    win_max, win_total, win_out = win_parts
    rand_max, rand_total, rand_out = rand_parts
    joint_max = jnp.maximum(win_max, jnp.max(rand_max, axis=2))
    win_scale = jnp.exp(win_max - joint_max)
    rand_scale = jnp.exp(rand_max - joint_max[:, :, None])
    numerator = win_scale[..., None] * win_out + jnp.sum(rand_scale[..., None] * rand_out, axis=2)
    denominator = win_scale * win_total + jnp.sum(rand_scale * rand_total, axis=2)
    return (numerator / denominator[..., None]).astype(jnp.bfloat16)


def head_blocks(rows):
    return rows.reshape(-1, BLK, HEADS, rows.shape[1] // HEADS).transpose(0, 2, 1, 3)


def per_device(
    tokens,
    w_query,
    w_key,
    w_value,
    w_out,
    norm_gain,
    norm_bias,
    w_pool,
    pool_bias,
    random_ids,
    lengths,
):
    shards = lax.axis_size("ctx")
    own_index = lax.axis_index("ctx")
    tok_rows, model_width = tokens.shape
    head_dim = model_width // HEADS
    blocks = tok_rows // BLK
    seq_total = tok_rows * shards
    first_block = own_index * blocks
    doc_ends = jnp.cumsum(lengths)
    queries = jnp.dot(tokens, w_query, preferred_element_type=jnp.float32).astype(jnp.bfloat16)
    keys_rows = jnp.dot(tokens, w_key, preferred_element_type=jnp.float32).astype(jnp.bfloat16)
    values_rows = jnp.dot(tokens, w_value, preferred_element_type=jnp.float32).astype(jnp.bfloat16)
    query_blocks = head_blocks(queries)
    keys_blocks = head_blocks(keys_rows)
    values_blocks = head_blocks(values_rows)
    paired = jnp.concatenate((keys_rows, values_rows), axis=1)
    paired_ext = with_halo(paired, (("ctx", 0),), BLK)
    keys_ext = paired_ext[:, :model_width]
    values_ext = paired_ext[:, model_width:]
    keys_ext_blocks = head_blocks(keys_ext)
    values_ext_blocks = head_blocks(values_ext)
    window_keys = jnp.concatenate(
        (keys_ext_blocks[:-2], keys_ext_blocks[1:-1], keys_ext_blocks[2:]), axis=2
    )
    window_values = jnp.concatenate(
        (values_ext_blocks[:-2], values_ext_blocks[1:-1], values_ext_blocks[2:]), axis=2
    )
    block_ids = first_block + jnp.arange(blocks, dtype=jnp.int32)
    query_pos = block_ids[:, None, None] * BLK + jnp.arange(BLK, dtype=jnp.int32)
    window_pos = (block_ids - 1)[:, None, None] * BLK + jnp.arange(3 * BLK, dtype=jnp.int32)
    win_parts = partial_attention(
        query_blocks, window_keys, window_values, query_pos, window_pos, doc_ends, seq_total, True
    )
    requests = HEADS * blocks * RAND
    capacity = max(2, (5 * requests + 4 * shards - 1) // (4 * shards))
    wanted = random_ids.reshape(requests)
    owners = wanted // blocks
    local_block = wanted % blocks
    one_hot = (owners[:, None] == jnp.arange(shards, dtype=jnp.int32)[None, :]).astype(jnp.int32)
    slot_index = jnp.sum((jnp.cumsum(one_hot, axis=0) - one_hot) * one_hot, axis=1)
    placed = owners * capacity + slot_index
    request_ids = jnp.arange(requests, dtype=jnp.int32)
    source = jnp.full((shards * capacity,), requests, jnp.int32).at[placed].set(request_ids)
    filled = source < requests
    picked = jnp.minimum(source, requests - 1)
    head_of = picked // RAND % HEADS
    block_size = BLK * head_dim
    shape_five = (blocks, HEADS, RAND, BLK, head_dim)
    query_rows = query_blocks.reshape(blocks * HEADS, block_size)
    sent_queries = jnp.where(filled[:, None], query_rows[picked // RAND], 0).reshape(
        shards, capacity, block_size
    )
    sent_meta = jnp.stack(
        (head_of, local_block[picked], first_block + picked // (RAND * HEADS)), axis=1
    )
    sent_meta = jnp.where(filled[:, None], sent_meta, 0).reshape(shards, capacity, 3)
    got_queries = lax.all_to_all(sent_queries, "ctx", split_axis=0, concat_axis=0, tiled=True)
    got_meta = lax.all_to_all(sent_meta, "ctx", split_axis=0, concat_axis=0, tiled=True)
    count = got_queries.shape[1]
    heads_in = got_meta[..., 0]
    blocks_in = got_meta[..., 1]
    anchor = got_meta[..., 2]
    asked_queries = got_queries.reshape(shards, count, BLK, head_dim)
    asked_keys = keys_blocks[blocks_in, heads_in]
    asked_values = values_blocks[blocks_in, heads_in]
    asked_qpos = anchor[..., None] * BLK + jnp.arange(BLK, dtype=jnp.int32)
    asked_kpos = ((first_block + blocks_in) * BLK)[..., None] + jnp.arange(BLK, dtype=jnp.int32)
    row_max, row_total, partial_out = partial_attention(
        asked_queries, asked_keys, asked_values, asked_qpos, asked_kpos, doc_ends, seq_total, False
    )
    got_out = lax.all_to_all(
        partial_out.reshape(shards, count, block_size),
        "ctx",
        split_axis=0,
        concat_axis=0,
        tiled=True,
    )
    got_max = lax.all_to_all(row_max, "ctx", split_axis=0, concat_axis=0, tiled=True)
    got_total = lax.all_to_all(row_total, "ctx", split_axis=0, concat_axis=0, tiled=True)
    rand_max = got_max.reshape(shards * capacity, BLK)[placed].reshape(blocks, HEADS, RAND, BLK)
    rand_total = got_total.reshape(shards * capacity, BLK)[placed].reshape(blocks, HEADS, RAND, BLK)
    rand_out = got_out.reshape(shards * capacity, block_size)[placed].reshape(shape_five)
    rand_parts = (rand_max, rand_total, rand_out)
    attention = combine(win_parts, rand_parts)
    attn_rows = attention.transpose(0, 2, 1, 3).reshape(tok_rows, model_width)
    mixed = tokens.astype(jnp.float32) + jnp.dot(
        attn_rows, w_out, preferred_element_type=jnp.float32
    )
    centre = jnp.mean(mixed, axis=1, keepdims=True)
    spread = jnp.mean(jnp.square(mixed - centre), axis=1, keepdims=True)
    encoded = ((mixed - centre) * lax.rsqrt(spread + 1e-05) * norm_gain + norm_bias).astype(
        jnp.bfloat16
    )
    starts = doc_ends - lengths
    positions = own_index * tok_rows + jnp.arange(tok_rows, dtype=jnp.int32)
    chooser = (starts[:, None] == positions[None, :]).astype(jnp.bfloat16)
    local_rows = jnp.dot(chooser, encoded, preferred_element_type=jnp.float32)
    pooled = lax.psum(local_rows.astype(jnp.bfloat16), "ctx")
    doc_vectors = jnp.tanh(jnp.dot(pooled, w_pool, preferred_element_type=jnp.float32) + pool_bias)
    return (encoded, doc_vectors)


def solution(mesh):
    placed = (
        P(("dp", "ctx"), None),
        P(),
        P(),
        P(),
        P(),
        P(),
        P(),
        P(),
        P(),
        P(("dp", "ctx"), None, None),
        P("dp"),
    )
    return jax.shard_map(
        per_device,
        mesh=mesh,
        in_specs=placed,
        out_specs=(P(("dp", "ctx"), None), P("dp", None)),
        check_vma=False,
    )
```

profile of v0, /device:TPU:1, one launch (start us, length us, event | category | flops | bytes accessed | tf_op | source)
XLA Modules:
  0.0 342.5 jit_solution(10397523645476951693)
XLA Ops:
  4.3 2.0 gather_fusion
  7.5 9.4 %all-to-all-start = ((s32[32,8,3]{1,2,0:T(4,128)}), s32[32,8,3]{1,2,0:T(4,128)S(1)}, u32[]{:S(2)}, u32[]{:S(2)}) async-start(s32[32,8,3]{1,2,0:T(4,128)} %copy.74), calls=%async_computation | async-start | bytes 131072 | tf_op jit(solution)/shard_map/all_to_all | solution.py:147
  16.9 3.3 convolution_convert_fusion.2
  20.2 1.8 reshape.387
  22.0 1.3 copy.93
  23.3 2.1 reshape.393
  25.3 3.2 gather_fusion.1
  28.5 3.2 bitcast_select_fusion
  31.7 7.5 %all-to-all-start.1 = ((bf16[32,8,4096]{2,1,0:T(8,128)(2,1)}), bf16[32,8,4096]{2,1,0:T(8,128)(2,1)}, u32[]{:S(2)}, u32[]{:S(2)}) async-start(bf16[32,8,4096]{2,1,0:T(8,128)(2,1)} %bitcast_select_fusion), calls=%async_computation.1 | async-start | bytes 4194304 | tf_op jit(solution)/shard_map/all_to_all | solution.py:146
  39.2 2.3 convolution_convert_fusion.1
  42.3 1.7 reshape.395
  44.0 1.5 copy.92
  45.5 3.3 convolution_convert_fusion
  49.0 3.3 gather_fusion.2
  52.4 15.2 %all-to-all-done.1 = bf16[32,8,4096]{2,1,0:T(8,128)(2,1)} async-done(((bf16[32,8,4096]{2,1,0:T(8,128)(2,1)}), bf16[32,8,4096]{2,1,0:T(8,128)(2,1)}, u32[]{:S(2)}, u32[]{:S(2)}) %all-to-all-start.1) | async-done | bytes 2097184 | tf_op jit(solution)/shard_map/all_to_all | solution.py:146
  67.6 6.9 %reshape.394 = bf16[32,8,64,64]{3,2,1,0:T(8,128)(2,1)} reshape(bf16[32,8,4096]{2,1,0:T(8,128)(2,1)} %all-to-all-done.1) | data formatting | bytes 4194304 | tf_op jit(solution)/shard_map/reshape | solution.py:152
  74.5 5.4 %fusion = (f32[32,8,64]{2,1,0:T(8,128)S(1)}, f32[32,8,64,64]{2,3,1,0:T(8,128)S(1)}) fusion(pred[32,8,64]{2,1,0:T(8,128)(4,1)S(1)} %fusion.38, bf16[32,8,64,64]{3,2,1,0:T(8,128)(2,1)} %reshape.394, bf16[32,8,64,64]{3,2,1,0:T(8,128)(2,1)} %bitcast.84), kind=kOutput, calls=%fused_computation.10 | convolution fusion | flops 137347072 | bytes 8470528 | tf_op jit(solution)/shard_map/...qd,...kd->...qk/dot_general | solution.py:40
  79.8 3.2 copy-done.1
  83.1 3.7 %fusion.1 = f32[32,8,64]{2,1,0:T(8,128)S(1)} fusion(f32[32,8,64,64]{2,3,1,0:T(8,128)S(1)} %get-tuple-element.25, f32[32,8,64]{2,1,0:T(8,128)S(1)} %get-tuple-element.24, pred[32,8,64]{2,1,0:T(8,128)(4,1)S(1)} %fusion.38), kind=kLoop, calls=%fused_computation.11 | loop fusion | flops 4177920 | bytes 4341760 | tf_op jit(solution)/shard_map/reduce_sum | solution.py:53
  87.6 4.3 %all-to-all-start.4 = ((f32[32,1,512]{2,1,0:T(1,128)}), f32[32,1,512]{2,1,0:T(1,128)S(1)}, u32[]{:S(2)}, u32[]{:S(2)}) async-start(f32[32,1,512]{2,1,0:T(1,128)} %reshape.481), calls=%async_computation.4 | async-start | bytes 131072 | tf_op jit(solution)/shard_map/all_to_all | solution.py:168
  92.7 2.2 collective-permute-start.1
  95.0 3.3 collective-permute-start
  98.3 1.7 reshape.399
  100.0 1.5 copy.91
  101.5 3.3 gather_fusion.4
  105.6 9.0 %all-to-all-start.2 = ((f32[32,1,512]{2,1,0:T(1,128)}), f32[32,1,512]{2,1,0:T(1,128)S(1)}, u32[]{:S(2)}, u32[]{:S(2)}) async-start(f32[32,1,512]{2,1,0:T(1,128)} %reshape.479), calls=%async_computation.2 | async-start | bytes 131072 | tf_op jit(solution)/shard_map/all_to_all | solution.py:167
  114.7 10.6 %fusion.3 = f32[32,8,64,64]{3,2,1,0:T(8,128)} fusion(bf16[32,8,64,64]{3,2,1,0:T(8,128)(2,1)} %bitcast.83, f32[32,8,64,64]{2,3,1,0:T(8,128)} %copy-done.1, f32[32,8,64]{2,1,0:T(8,128)S(1)} %get-tuple-element.24, pred[32,8,64]{2,1,0:T(8,128)(4,1)S(1)} %fusion.38), kind=kOutput, calls=%fused_computation.14 | convolution fusion | flops 138412032 | bytes 10567680 | tf_op jit(solution)/shard_map/...qk,...kd->...qd/dot_general | solution.py:54
  125.3 7.9 %reshape.400 = f32[32,8,4096]{2,1,0:T(8,128)} reshape(f32[32,8,64,64]{3,2,1,0:T(8,128)} %fusion.3) | data formatting | bytes 8388608 | tf_op jit(solution)/shard_map/reshape | solution.py:161
  133.8 7.4 %all-to-all-start.3 = ((f32[32,8,4096]{2,1,0:T(8,128)}), f32[32,8,4096]{2,1,0:T(8,128)}, u32[]{:S(2)}, u32[]{:S(2)}) async-start(f32[32,8,4096]{2,1,0:T(8,128)} %reshape.400), calls=%async_computation.3 | async-start | bytes 8388608 | tf_op jit(solution)/shard_map/all_to_all | solution.py:160
  144.3 3.2 reshape.388
  147.5 3.2 copy.65
  150.7 1.9 reshape.398
  152.6 3.2 copy.76
  155.8 2.8 fusion.65
  158.6 2.1 fusion.63
  160.7 2.0 fusion.9
  162.8 1.9 copy-done.8
  164.7 2.1 fusion.10
  169.0 1.6 reduce.9
  173.1 20.2 %all-to-all-done.3 = f32[32,8,4096]{2,1,0:T(8,128)} async-done(((f32[32,8,4096]{2,1,0:T(8,128)}), f32[32,8,4096]{2,1,0:T(8,128)}, u32[]{:S(2)}, u32[]{:S(2)}) %all-to-all-start.3) | async-done | bytes 4194336 | tf_op jit(solution)/shard_map/all_to_all | solution.py:160
  193.4 6.8 %gather_fusion.5 = f32[192,4096]{1,0:T(8,128)} fusion(f32[256,4096]{1,0:T(8,128)} %bitcast.18, s32[1024]{0:T(1024)S(1)} %pad_clamp_fusion), kind=kCustom, calls=%fused_computation.5 | custom fusion | bytes 6292224 | tf_op jit(solution)/shard_map/gather | solution.py:171
  200.1 6.1 %reshape.402 = f32[4,16,3,64,64]{4,3,2,1,0:T(8,128)} reshape(f32[192,4096]{1,0:T(8,128)} %gather_fusion.5) | data formatting | bytes 6291456 | tf_op jit(solution)/shard_map/reshape | solution.py:171
  206.2 5.4 %multiply_reduce_fusion = f32[4,16,64,64]{3,2,1,0:T(8,128)S(1)} fusion(f32[4,16,3,64,64]{4,3,2,1,0:T(8,128)} %reshape.402, f32[4,16,3,64]{3,2,1,0:T(4,128)S(1)} %get-tuple-element.5), kind=kLoop, calls=%fused_computation.13 | loop fusion | flops 1310720 | bytes 4243456 | tf_op jit(solution)/shard_map/reduce_sum | solution.py:69
  211.7 3.3 fusion.26
  215.7 1.5 reshape.405
  217.2 2.0 fusion.66
  220.0 119.9 %psum.7 = bf16[8,1024]{1,0:T(8,128)(2,1)S(1)} all-reduce(bf16[8,1024]{1,0:T(8,128)(2,1)S(1)} %convolution_convert_fusion.3), channel_id=1, replica_groups=mesh['dp'=4,'ctx'=32] {'ctx'}, use_global_device_ids=true, to_apply=%region_16.17 | all-reduce | flops 8192 | bytes 32768 | tf_op jit(solution)/shard_map/psum | solution.py:187
  339.9 2.6 fusion.31
  (121 shorter events, 17.9 us)
Async XLA Ops:
  0.6 216.6 %copy-start = (bf16[1024,1024]{1,0:T(8,128)(2,1)S(1)}, bf16[1024,1024]{1,0:T(8,128)(2,1)}, u32[]{:S(2)}) copy-start(bf16[1024,1024]{1,0:T(8,128)(2,1)} %param.15) | copy-start | bytes 6291460
  7.5 24.2 %all-to-all-start = ((s32[32,8,3]{1,2,0:T(4,128)}), s32[32,8,3]{1,2,0:T(4,128)S(1)}, u32[]{:S(2)}, u32[]{:S(2)}) async-start(s32[32,8,3]{1,2,0:T(4,128)} %copy.74), calls=%async_computation | async-start | bytes 131072 | tf_op jit(solution)/shard_map/all_to_all | solution.py:147
  21.9 1.3 copy-start.10
  28.5 10.7 %copy-start.15 = (bf16[256,1024]{1,0:T(8,128)(2,1)S(1)}, bf16[256,1024]{1,0:T(8,128)(2,1)}, u32[]{:S(2)}) copy-start(bf16[256,1024]{1,0:T(8,128)(2,1)} %param.11) | copy-start | bytes 1572868
  31.7 35.8 %all-to-all-start.1 = ((bf16[32,8,4096]{2,1,0:T(8,128)(2,1)}), bf16[32,8,4096]{2,1,0:T(8,128)(2,1)}, u32[]{:S(2)}, u32[]{:S(2)}) async-start(bf16[32,8,4096]{2,1,0:T(8,128)(2,1)} %bitcast_select_fusion), calls=%async_computation.1 | async-start | bytes 4194304 | tf_op jit(solution)/shard_map/all_to_all | solution.py:146
  41.5 0.8 copy-start.3
  79.8 3.2 copy-start.1
  83.1 8.8 %copy-start.4 = (bf16[256,1024]{1,0:T(8,128)(2,1)S(1)}, bf16[256,1024]{1,0:T(8,128)(2,1)}, u32[]{:S(2)}) copy-start(bf16[256,1024]{1,0:T(8,128)(2,1)} %copy-done.3) | copy-start | bytes 1572868
  83.1 8.8 %copy-start.6 = (bf16[256,1024]{1,0:T(8,128)(2,1)S(1)}, bf16[256,1024]{1,0:T(8,128)(2,1)}, u32[]{:S(2)}) copy-start(bf16[256,1024]{1,0:T(8,128)(2,1)} %convolution_convert_fusion) | copy-start | bytes 1572868
  87.6 18.1 %all-to-all-start.4 = ((f32[32,1,512]{2,1,0:T(1,128)}), f32[32,1,512]{2,1,0:T(1,128)S(1)}, u32[]{:S(2)}, u32[]{:S(2)}) async-start(f32[32,1,512]{2,1,0:T(1,128)} %reshape.481), calls=%async_computation.4 | async-start | bytes 131072 | tf_op jit(solution)/shard_map/all_to_all | solution.py:168
  92.7 49.3 %collective-permute-start.1 = (bf16[64,2048]{1,0:T(8,128)(2,1)}, bf16[64,2048]{1,0:T(8,128)(2,1)}, u32[]{:S(2)}, u32[]{:S(2)}) collective-permute-start(bf16[64,2048]{1,0:T(8,128)(2,1)} %get-tuple-element.17), channel_id=1, source_target_pairs={{1,0},{2,1},{3,2},{4,3},{5,4},{6,5},{7,6},{8,7},{9,8},{10,9},{11,1... | collective-permute-start | bytes 786440 | tf_op jit(solution)/shard_map/ppermute | solution.py:24
  95.0 47.0 %collective-permute-start = (bf16[64,2048]{1,0:T(8,128)(2,1)}, bf16[64,2048]{1,0:T(8,128)(2,1)}, u32[]{:S(2)}, u32[]{:S(2)}) collective-permute-start(bf16[64,2048]{1,0:T(8,128)(2,1)} %get-tuple-element.16), channel_id=1, source_target_pairs={{0,1},{1,2},{2,3},{3,4},{4,5},{5,6},{6,7},{7,8},{8,9},{9,10},{10,1... | collective-permute-start | bytes 786440 | tf_op jit(solution)/shard_map/ppermute | solution.py:22
  105.6 27.6 %all-to-all-start.2 = ((f32[32,1,512]{2,1,0:T(1,128)}), f32[32,1,512]{2,1,0:T(1,128)S(1)}, u32[]{:S(2)}, u32[]{:S(2)}) async-start(f32[32,1,512]{2,1,0:T(1,128)} %reshape.479), calls=%async_computation.2 | async-start | bytes 131072 | tf_op jit(solution)/shard_map/all_to_all | solution.py:167
  133.2 8.1 %copy-start.25 = (s32[8]{0:T(128)S(1)}, s32[8]{0:T(128)}, u32[]{:S(2)}) copy-start(s32[8]{0:T(128)} %param.21) | copy-start | bytes 100
  133.2 8.9 %copy-start.5 = (bf16[256,1024]{1,0:T(8,128)(2,1)S(1)}, bf16[256,1024]{1,0:T(8,128)(2,1)}, u32[]{:S(2)}) copy-start(bf16[256,1024]{1,0:T(8,128)(2,1)} %copy-done.3) | copy-start | bytes 1572868
  133.2 8.9 %copy-start.7 = (bf16[256,1024]{1,0:T(8,128)(2,1)S(1)}, bf16[256,1024]{1,0:T(8,128)(2,1)}, u32[]{:S(2)}) copy-start(bf16[256,1024]{1,0:T(8,128)(2,1)} %convolution_convert_fusion) | copy-start | bytes 1572868
  133.2 0.6 copy-start.21
  133.8 59.6 %all-to-all-start.3 = ((f32[32,8,4096]{2,1,0:T(8,128)}), f32[32,8,4096]{2,1,0:T(8,128)}, u32[]{:S(2)}, u32[]{:S(2)}) async-start(f32[32,8,4096]{2,1,0:T(8,128)} %reshape.400), calls=%async_computation.3 | async-start | bytes 8388608 | tf_op jit(solution)/shard_map/all_to_all | solution.py:160
  142.0 20.8 %copy-start.19 = (pred[4,64,192]{2,1,0:T(8,128)(4,1)}, pred[4,64,192]{2,1,0:T(8,128)(4,1)S(1)}, u32[]{:S(2)}) copy-start(pred[4,64,192]{2,1,0:T(8,128)(4,1)S(1)} %compare_and_fusion) | copy-start | bytes 147460
  155.8 2.8 copy-start.2
  158.6 2.1 copy-start.11
  162.7 2.0 copy-start.8
  162.7 8.8 %copy-start.16 = (f32[4,16,64]{2,1,0:T(8,128)}, f32[4,16,64]{2,1,0:T(8,128)S(1)}, u32[]{:S(2)}) copy-start(f32[4,16,64]{2,1,0:T(8,128)S(1)} %get-tuple-element.26) | copy-start | bytes 49156
  171.6 0.6 copy-start.18
  206.2 5.4 %copy-start.9 = (f32[4,16,64,192]{3,2,1,0:T(8,128)S(1)}, f32[4,16,64,192]{3,2,1,0:T(8,128)}, u32[]{:S(2)}) copy-start(f32[4,16,64,192]{3,2,1,0:T(8,128)} %copy-done.8) | copy-start | bytes 9437188
  206.2 5.4 %copy-start.13 = (bf16[4,16,64,64]{2,3,1,0:T(8,128)(2,1)S(1)}, bf16[4,16,64,64]{2,3,1,0:T(8,128)(2,1)}, u32[]{:S(2)}) copy-start(bf16[4,16,64,64]{2,3,1,0:T(8,128)(2,1)} %get-tuple-element.9) | copy-start | bytes 1572868
  206.2 5.4 %copy-start.14 = (bf16[4,16,64,64]{2,3,1,0:T(8,128)(2,1)S(1)}, bf16[4,16,64,64]{2,3,1,0:T(8,128)(2,1)}, u32[]{:S(2)}) copy-start(bf16[4,16,64,64]{2,3,1,0:T(8,128)(2,1)} %get-tuple-element.10) | copy-start | bytes 1572868
  206.2 5.5 %copy-start.17 = (f32[4,16,64]{2,1,0:T(8,128)S(1)}, f32[4,16,64]{2,1,0:T(8,128)}, u32[]{:S(2)}) copy-start(f32[4,16,64]{2,1,0:T(8,128)} %copy-done.16) | copy-start | bytes 49156
  206.2 5.5 %copy-start.20 = (pred[4,64,192]{2,1,0:T(8,128)(4,1)S(1)}, pred[4,64,192]{2,1,0:T(8,128)(4,1)}, u32[]{:S(2)}) copy-start(pred[4,64,192]{2,1,0:T(8,128)(4,1)} %copy-done.19) | copy-start | bytes 147460
  215.0 4.5 %copy-start.22 = (f32[1024]{0:T(1024)S(1)}, f32[1024]{0:T(1024)}, u32[]{:S(2)}) copy-start(f32[1024]{0:T(1024)} %param.17) | copy-start | bytes 12292
  215.0 4.5 %copy-start.23 = (f32[1024]{0:T(1024)S(1)}, f32[1024]{0:T(1024)}, u32[]{:S(2)}) copy-start(f32[1024]{0:T(1024)} %param.16) | copy-start | bytes 12292
  215.7 124.2 %copy-start.24 = (f32[1024]{0:T(1024)S(1)}, f32[1024]{0:T(1024)}, u32[]{:S(2)}) copy-start(f32[1024]{0:T(1024)} %param.19) | copy-start | bytes 12292
  219.8 122.7 %copy-start.12 = (bf16[256,1024]{1,0:T(8,128)(2,1)}, bf16[256,1024]{1,0:T(8,128)(2,1)S(1)}, u32[]{:S(2)}) copy-start(bf16[256,1024]{1,0:T(8,128)(2,1)S(1)} %add_convert_fusion) | copy-start | bytes 1572868
where the time goes:
time: 348 us; the launch traced here: 343 us
  blocking collectives  120 us (34%)
  local copies, waits for them, and re-layouts  85.6 us (25%)
  starting transfers between devices  43.2 us (12%)
  waiting for transfers between devices  35.4 us (10%)
  matrix products  34.9 us (10%)
  other arithmetic  22.2 us (6%)
    psum x1, blocking collectives, per_device(): pooled = lax.psum(local_rows.astype(jnp.bfloat16), 'ctx')  120 us
    reshape x10, local copies, waits for them, and re-layouts, head_blocks(): rows.reshape(-1, BLK, HEADS, rows.shape[1] // HEADS).transpose(0, 2, 1, 3)  21 us
    all_to_all x1, waiting for transfers between devices, per_device(): lax.all_to_all(partial_out.reshape(shards, count, block_size), 'ctx', spl...  20.2 us
    all_to_all x1, waiting for transfers between devices, per_device(): lax.all_to_all(sent_queries, 'ctx', split_axis=0, concat_axis=0, tiled=True)  15.2 us
    dot_general x2, matrix products, partial_attention(): jnp.einsum('...qk,...kd->...qd', weights.astype(jnp.bfloat16), values_in,...  13.9 us
    unnamed x57, local copies, waits for them, and re-layouts  9.87 us
    all_to_all x1, starting transfers between devices, per_device(): lax.all_to_all(sent_meta, 'ctx', split_axis=0, concat_axis=0, tiled=True)  9.42 us
    all_to_all x1, starting transfers between devices, per_device(): lax.all_to_all(row_max, 'ctx', split_axis=0, concat_axis=0, tiled=True)  9.05 us
  transfers between devices with their start and end apart: 7, of which 2 were waited for; matrix products, arithmetic and copies ran while one was open for 24% of the time, Pallas kernels for 0%

commit v1 on v0

v1 whole, which is shorter than its diff:
```python
import jax
import jax.numpy as jnp
from jax import lax
from jax.experimental import pallas as pl
from jax.experimental.pallas import tpu as pltpu
from jax.sharding import PartitionSpec as P

HEADS = 16
BLK = 64
RAND = 3
DOCS = 8
D = 1024
ROWS = 256
SEQ = 8192
NBLK = 128
SIDE = 4
CHIPS = 16
SHARDS = 32
IDS = HEADS * RAND * (ROWS // BLK)
KEYS = 6 * BLK
QROWS = 144

MESH = pl.DeviceIdType.MESH
BF = jnp.bfloat16
F32 = jnp.float32
MASKED = -240000.0
EXP_SCALE = 0.125 * 1.4426950408889634


def turn(a):
    return a + (a // 2) * (1 - 2 * (a % 2))


def kernel(
    ids_ref, len_ref, tok_ref, gain_ref, bias_ref, pbias_ref,
    wq_hbm, wk_hbm, wv_hbm, wo_hbm, wp_hbm,
    enc_ref, doc_ref,
    wq, wk, wv, wo, wp,
    kv_send, kv_buf, q_send, q_recv, att_send, att_recv, doc_send, doc_recv,
    ids_recv, ids_smem, lhs, mixed,
    w_sem, own_sem, ids_ss, ids_rs, kv_ss, kv_rs, sib_ss, sib_rs,
    q_ss, q_rs, att_ss, att_rs, doc_ss, doc_rs,
):
    dp = lax.axis_index("dp")
    me = lax.axis_index("ctx")
    core = me % 2
    chip = me // 2
    cx = chip // SIDE
    cz = chip % SIDE

    def chip_at(k, sign):
        dx, dz = turn(k // SIDE), turn(k % SIDE)
        return ((cx + sign * dx + SIDE) % SIDE) * SIDE + (cz + sign * dz + SIDE) % SIDE

    def to_ctx(c):
        return (dp, 2 * c + core)

    sibling = (dp, 2 * chip + 1 - core)

    barrier = pltpu.get_barrier_semaphore()

    def greet(j, carry):
        pl.semaphore_signal(
            barrier, inc=1, device_id=(dp, (me + j) % SHARDS), device_id_type=MESH
        )
        return carry

    lax.fori_loop(1, SHARDS, greet, 0)

    def load(hbm, vmem, n):
        return pltpu.make_async_copy(hbm, vmem, w_sem.at[n])

    loads = [
        load(wk_hbm, wk, 0), load(wv_hbm, wv, 1), load(wq_hbm, wq, 2),
        load(wo_hbm, wo, 3), load(wp_hbm, wp, 4),
    ]
    for copy in loads:
        copy.start()

    lane = lax.broadcasted_iota(jnp.int32, (1, 128), 1)
    low = lane < 64

    def interleave(first, second):
        return (
            jnp.where(low, first, pltpu.roll(second, 64, 1)),
            jnp.where(low, pltpu.roll(first, 64, 1), second),
        )

    ends, starts = [], []
    total = jnp.int32(0)
    for d in range(DOCS):
        starts.append(total)
        total = total + len_ref[d]
        ends.append(total)

    def rows_of(i):
        return pl.ds(4 * i + 1, 4)

    loads[0].wait()
    loads[1].wait()

    def kv_step(g, carry):
        cols = pl.ds(pl.multiple_of(g * 256, 256), 256)
        k = jnp.dot(tok_ref[...], wk[:, cols], preferred_element_type=F32)
        v = jnp.dot(tok_ref[...], wv[:, cols], preferred_element_type=F32)
        for p in range(2):
            s = slice(128 * p, 128 * p + 128)
            even, odd = interleave(k[:, s], v[:, s])
            kv_send[4 * g + 2 * p] = even.astype(BF).reshape(4, BLK, 128)
            kv_send[4 * g + 2 * p + 1] = odd.astype(BF).reshape(4, BLK, 128)
        return carry

    lax.fori_loop(0, 4, kv_step, 0)

    pl.semaphore_wait(barrier, SHARDS - 1)

    def ids_copy(k):
        return pltpu.make_async_remote_copy(
            src_ref=ids_ref, dst_ref=ids_recv.at[chip], send_sem=ids_ss.at[k],
            recv_sem=ids_rs.at[k], device_id=to_ctx(chip_at(k, 1)), device_id_type=MESH,
        )

    def kv_copy(k):
        c = chip_at(k, 1)
        return pltpu.make_async_remote_copy(
            src_ref=kv_send.at[c], dst_ref=kv_buf.at[rows_of(me)], send_sem=kv_ss.at[k],
            recv_sem=kv_rs.at[k], device_id=to_ctx(c), device_id_type=MESH,
        )

    def q_copy(k):
        c = chip_at(k, 1)
        return pltpu.make_async_remote_copy(
            src_ref=q_send.at[c], dst_ref=q_recv.at[k], send_sem=q_ss.at[k],
            recv_sem=q_rs.at[k], device_id=to_ctx(c), device_id_type=MESH,
        )

    def att_copy(k):
        c = chip_at(k, -1)
        return pltpu.make_async_remote_copy(
            src_ref=att_send.at[c], dst_ref=att_recv.at[chip], send_sem=att_ss.at[k],
            recv_sem=att_rs.at[k], device_id=to_ctx(c), device_id_type=MESH,
        )

    def sib_own():
        return pltpu.make_async_remote_copy(
            src_ref=kv_send.at[chip], dst_ref=kv_buf.at[rows_of(me)],
            send_sem=sib_ss.at[0], recv_sem=sib_rs.at[0], device_id=sibling,
            device_id_type=MESH,
        )

    def sib_copy(k):
        rows = rows_of(2 * chip_at(k, -1) + core)
        return pltpu.make_async_remote_copy(
            src_ref=kv_buf.at[rows], dst_ref=kv_buf.at[rows],
            send_sem=sib_ss.at[k], recv_sem=sib_rs.at[k], device_id=sibling,
            device_id_type=MESH,
        )

    def doc_copy(j):
        return pltpu.make_async_remote_copy(
            src_ref=doc_send, dst_ref=doc_recv.at[me], send_sem=doc_ss.at[j],
            recv_sem=doc_rs.at[j], device_id=(dp, (me + j) % SHARDS), device_id_type=MESH,
        )

    def loop(lo, hi, body):
        def step(k, carry):
            body(k)
            return carry
        lax.fori_loop(lo, hi, step, 0)

    loop(1, CHIPS, lambda k: ids_copy(k).start())
    loop(1, CHIPS, lambda k: kv_copy(k).start())
    sib_own().start()
    own_kv = pltpu.make_async_copy(kv_send.at[chip], kv_buf.at[rows_of(me)], own_sem.at[0])
    own_kv.start()
    own_ids = pltpu.make_async_copy(ids_ref, ids_recv.at[chip], own_sem.at[1])
    own_ids.start()

    first_row = me * ROWS
    pick_row = lax.broadcasted_iota(jnp.int32, (16, 1), 0)
    pick = jnp.full((16, 1), -1, jnp.int32)
    for d in range(DOCS):
        pick = jnp.where(pick_row == d, starts[d], pick)
    pos = first_row + lax.broadcasted_iota(jnp.int32, (1, ROWS), 1)
    chooser = jnp.where(pick == pos, 1.0, 0.0).astype(BF)

    loads[2].wait()

    def q_step(g, carry):
        cols = pl.ds(pl.multiple_of(g * 256, 256), 256)
        q = jnp.dot(tok_ref[...], wq[:, cols], preferred_element_type=F32)
        t = jnp.dot(chooser, tok_ref[:, cols], preferred_element_type=F32)
        for p in range(2):
            s = slice(128 * p, 128 * p + 128)
            even, odd = interleave(q[:128, s], q[128:, s])
            q_send[4 * g + 2 * p, 0:128, :] = even.astype(BF)
            q_send[4 * g + 2 * p + 1, 0:128, :] = odd.astype(BF)
            q_send[4 * g + 2 * p, 128:QROWS, :] = t[:, s].astype(BF)
            q_send[4 * g + 2 * p + 1, 128:QROWS, :] = pltpu.roll(t[:, s], 64, 1).astype(BF)
        return carry

    lax.fori_loop(0, 4, q_step, 0)
    loop(1, CHIPS, lambda k: q_copy(k).start())
    own_q = pltpu.make_async_copy(q_send.at[chip], q_recv.at[0], own_sem.at[2])
    own_q.start()

    kv_buf[0] = jnp.zeros((BLK, 128), BF)
    kv_buf[NBLK + 1] = jnp.zeros((BLK, 128), BF)

    def pass_on(k):
        kv_copy(k).wait_recv()
        sib_copy(k).start()

    loop(1, CHIPS, pass_on)
    loop(1, CHIPS, lambda k: ids_copy(k).wait_recv())
    own_ids.wait()
    to_smem = pltpu.make_async_copy(ids_recv, ids_smem, own_sem.at[3])
    to_smem.start()
    to_smem.wait()
    own_kv.wait()
    sib_own().wait_recv()
    loop(1, CHIPS, lambda k: sib_copy(k).wait_recv())

    col = lax.broadcasted_iota(jnp.int32, (1, KEYS), 1)
    row = lax.broadcasted_iota(jnp.int32, (BLK, 1), 0)

    def doc_of(positions):
        found = jnp.zeros(positions.shape, jnp.int32)
        for d in range(DOCS):
            found = found + jnp.where(positions >= ends[d], 1, 0)
        return found

    def attend(k):
        c = chip_at(k, -1)
        first = (2 * c + core) * (ROWS // BLK)

        @pl.when(k == 0)
        def _():
            own_q.wait()

        @pl.when(k > 0)
        def _():
            q_copy(k).wait_recv()

        for j in range(2):
            outs = []
            pair = q_recv[k, BLK * j:BLK * j + BLK, :].astype(F32)
            for half in range(2):
                block = j + 2 * half
                b = first + block
                q = pltpu.roll(pair, 64, 1) if half else pair
                q = jnp.where(low, q, 0.0).astype(BF)
                parts = [kv_buf[pl.ds(b, 3)].reshape(3 * BLK, 128)]
                for r in range(RAND):
                    at = ids_smem[c, 0, block * HEADS * RAND + chip * RAND + r]
                    parts.append(kv_buf[at + 1])
                kv = jnp.concatenate(parts, axis=0)
                s = lax.dot_general(
                    q, kv, (((1,), (1,)), ((), ())), preferred_element_type=F32
                )
                kpos = (b - 1) * BLK + col
                kdoc = jnp.where((kpos < 0) | (kpos >= SEQ), -1, doc_of(kpos))
                qdoc = doc_of(b * BLK + row)
                keep = (qdoc == kdoc) | (col >= 3 * BLK)
                s = jnp.where(keep, s, MASKED)
                m = jnp.max(s, axis=1, keepdims=True)
                w = jnp.exp2((s - m) * EXP_SCALE)
                l = jnp.sum(w, axis=1, keepdims=True)
                o = jnp.dot(w.astype(BF), kv, preferred_element_type=F32)
                outs.append(o / l)
            att_send[c, 4 * j:4 * j + 4] = jnp.where(
                low, pltpu.roll(outs[0], 64, 1), outs[1]
            ).astype(BF).reshape(4, 16, 128)

        @pl.when(k > 0)
        def _():
            att_copy(k).start()

    loop(0, CHIPS, attend)
    own_att = pltpu.make_async_copy(att_send.at[chip], att_recv.at[chip], own_sem.at[4])
    own_att.start()

    tok_piece = jnp.zeros((16, 128), F32)
    for k in range(CHIPS):
        tok_piece = tok_piece + q_recv[k, 128:QROWS, :].astype(F32)
    att_piece = jnp.zeros((8, 128), F32)
    row8 = lax.broadcasted_iota(jnp.int32, (8, 1), 0)
    row16 = lax.broadcasted_iota(jnp.int32, (16, 1), 0)
    for d in range(DOCS):
        home = starts[d] // ROWS
        local = starts[d] % ROWS
        packed = local % 128
        tile = att_send[home // 2, packed // 16].astype(F32)
        here = row16 + 16 * core == packed % 16 + 16 * (home % 2)
        one = jnp.where(here, tile, 0.0)
        one = jnp.sum(one, axis=0, keepdims=True)
        one = jnp.where(lane * 0 + local >= 128, pltpu.roll(one, 64, 1), one)
        att_piece = jnp.where(row8 == d, one, att_piece)
    doc_send[...] = jnp.concatenate((att_piece, tok_piece[:8]), axis=0).astype(BF)
    loop(1, SHARDS, lambda j: doc_copy(j).start())

    loop(1, CHIPS, lambda k: att_copy(k).wait_recv())
    own_att.wait()
    loads[3].wait()
    for j in range(CHIPS // 2):
        even = att_recv[2 * j].reshape(128, 128).astype(F32)
        odd = att_recv[2 * j + 1].reshape(128, 128).astype(F32)
        top, bottom = interleave(even, odd)
        s = slice(128 * j, 128 * j + 128)
        lhs[0:128, s] = top.astype(BF)
        lhs[128:256, s] = bottom.astype(BF)
    loop(1, SHARDS, lambda j: doc_copy(j).wait_recv())
    doc_recv[me] = doc_send[...]
    pieces = [
        doc_recv[2 * h].astype(F32) + doc_recv[2 * h + 1].astype(F32) for h in range(CHIPS)
    ]
    for j in range(CHIPS // 2):
        both = jnp.where(low, pieces[2 * j], pltpu.roll(pieces[2 * j + 1], 64, 1))
        s = slice(128 * j, 128 * j + 128)
        lhs[256:272, s] = both.astype(BF)
        mixed[256:264, s] = both[8:]
    loads[4].wait()

    def out_step(n, carry):
        cols = pl.ds(pl.multiple_of(n * 256, 256), 256)
        y = jnp.dot(lhs[...], wo[:, cols], preferred_element_type=F32)
        mixed[0:256, cols] = tok_ref[:, cols].astype(F32) + y[:256]
        mixed[256:264, cols] = mixed[256:264, cols] + y[256:264]
        return carry

    lax.fori_loop(0, 4, out_step, 0)

    def normed(rows):
        centre = jnp.mean(rows, axis=1, keepdims=True)
        spread = jnp.mean(jnp.square(rows - centre), axis=1, keepdims=True)
        return ((rows - centre) * lax.rsqrt(spread + 1e-05) * gain_ref[...] + bias_ref[...]).astype(BF)

    def norm_step(n, carry):
        rows = pl.ds(pl.multiple_of(n * 64, 64), 64)
        enc_ref[rows, :] = normed(mixed[rows, :])
        return carry

    lax.fori_loop(0, 4, norm_step, 0)
    pooled = normed(mixed[256:264, :])
    doc_ref[...] = jnp.tanh(
        jnp.dot(pooled, wp[...], preferred_element_type=F32) + pbias_ref[...]
    )

    loop(1, CHIPS, lambda k: ids_copy(k).wait_send())
    loop(1, CHIPS, lambda k: kv_copy(k).wait_send())
    loop(1, CHIPS, lambda k: q_copy(k).wait_send())
    loop(1, CHIPS, lambda k: att_copy(k).wait_send())
    sib_own().wait_send()
    loop(1, CHIPS, lambda k: sib_copy(k).wait_send())
    loop(1, SHARDS, lambda j: doc_copy(j).wait_send())


def per_device(
    tokens, w_query, w_key, w_value, w_out, norm_gain, norm_bias, w_pool, pool_bias,
    random_ids, lengths,
):
    vmem = pl.BlockSpec(memory_space=pltpu.VMEM)
    smem = pl.BlockSpec(memory_space=pltpu.SMEM)
    hbm = pl.BlockSpec(memory_space=pl.ANY)
    ids = jnp.pad(random_ids.reshape(1, IDS), ((0, 0), (0, 256 - IDS)))
    dma = pltpu.SemaphoreType.DMA
    return pl.pallas_call(
        kernel,
        out_shape=(
            jax.ShapeDtypeStruct((ROWS, D), BF),
            jax.ShapeDtypeStruct((DOCS, D), F32),
        ),
        in_specs=[vmem, smem, vmem, vmem, vmem, vmem, hbm, hbm, hbm, hbm, hbm],
        out_specs=(vmem, vmem),
        scratch_shapes=[
            pltpu.VMEM((D, D), BF), pltpu.VMEM((D, D), BF), pltpu.VMEM((D, D), BF),
            pltpu.VMEM((D, D), BF), pltpu.VMEM((D, D), BF),
            pltpu.VMEM((CHIPS, 4, BLK, 128), BF),
            pltpu.VMEM((NBLK + 2, BLK, 128), BF),
            pltpu.VMEM((CHIPS, QROWS, 128), BF),
            pltpu.VMEM((CHIPS, QROWS, 128), BF),
            pltpu.VMEM((CHIPS, 8, 16, 128), BF),
            pltpu.VMEM((CHIPS, 8, 16, 128), BF),
            pltpu.VMEM((16, 128), BF),
            pltpu.VMEM((SHARDS, 16, 128), BF),
            pltpu.VMEM((CHIPS, 1, 256), jnp.int32),
            pltpu.SMEM((CHIPS, 1, 256), jnp.int32),
            pltpu.VMEM((272, D), BF),
            pltpu.VMEM((264, D), F32),
            dma((5,)), dma((5,)),
            dma((CHIPS,)), dma((CHIPS,)), dma((CHIPS,)), dma((CHIPS,)),
            dma((CHIPS,)), dma((CHIPS,)), dma((CHIPS,)), dma((CHIPS,)),
            dma((CHIPS,)), dma((CHIPS,)), dma((SHARDS,)), dma((SHARDS,)),
        ],
        compiler_params=pltpu.CompilerParams(
            collective_id=0, has_side_effects=True, vmem_limit_bytes=56 << 20
        ),
    )(
        ids, lengths, tokens, norm_gain.reshape(1, D), norm_bias.reshape(1, D),
        pool_bias.reshape(1, D), w_query, w_key, w_value, w_out, w_pool,
    )


def solution(mesh):
    rows = P(("dp", "ctx"), None)
    placed = (
        rows, P(), P(), P(), P(), P(), P(), P(), P(),
        P(("dp", "ctx"), None, None), P("dp"),
    )
    return jax.shard_map(
        per_device,
        mesh=mesh,
        in_specs=placed,
        out_specs=(rows, P("dp", None)),
        check_vma=False,
    )
```

time: 348 us -> 64.1 us (0.18); the launches traced: 343 us -> 63.8 us
  blocking collectives: 120 us -> 0 us
  local copies, waits for them, and re-layouts: 85.6 us -> 4.74 us
  Pallas kernels: 0 us -> 58.5 us
  starting transfers between devices: 43.2 us -> 0 us
  waiting for transfers between devices: 35.4 us -> 0 us
  matrix products: 34.9 us -> 0 us
  other arithmetic: 22.2 us -> 0 us
    psum x1 -> x0, blocking collectives: 120 us -> none  [per_device(): pooled = lax.psum(local_rows.astype(jnp.bfloat16), 'ctx')]
    pallas_call x0 -> x1, Pallas kernels: none -> 58.5 us  [per_device(): pl.pallas_call(kernel, out_shape=(jax.ShapeDtypeStruct((ROWS, D), BF), ja...]
    reshape x19 -> x1, local copies, waits for them, and re-layouts: 45.8 us -> 0.13 us  [per_device(): ids = jnp.pad(random_ids.reshape(1, IDS), ((0, 0), (0, 256 - IDS)))]
    all_to_all x5 -> x0, starting transfers between devices: 37.7 us -> none  [the longest x1 9.42 us: per_device(): lax.all_to_all(sent_meta, 'ctx', split_axis=0, concat_axis=0, tiled=True)]
    all_to_all x5 -> x0, waiting for transfers between devices: 35.4 us -> none  [the longest x1 20.2 us: per_device(): lax.all_to_all(partial_out.reshape(shards, count, block_size), 'ctx', spl...]
    dot_general x10 -> x0, matrix products: 34.9 us -> none  [the longest x2 13.9 us: partial_attention(): jnp.einsum('...qk,...kd->...qd', weights.astype(jnp.bfloat16), values_in,...]
    gather x7 -> x0, local copies, waits for them, and re-layouts: 19.9 us -> none  [the longest x1 6.76 us: per_device(): got_out.reshape(shards * capacity, block_size)[placed].reshape(shape_five)]
    reduce_sum x8 -> x0, other arithmetic: 11.9 us -> none  [the longest x2 5.88 us: partial_attention(): row_total = jnp.sum(weights, axis=-1)]
  transfers between devices with their start and end apart: 7 -> 0, of which waited for: 2 -> 0; matrix products, arithmetic and copies ran while one was open for 24% -> 0% of each run, Pallas kernels for 0% -> 0%
where the time goes in v1:
time: 64.1 us; the launch traced here: 63.8 us
  Pallas kernels  58.5 us (91%)
  local copies, waits for them, and re-layouts  4.74 us (7%)
    pallas_call x1, Pallas kernels, per_device(): pl.pallas_call(kernel, out_shape=(jax.ShapeDtypeStruct((ROWS, D), BF), ja...  58.5 us
    unnamed x3, local copies, waits for them, and re-layouts  4.03 us

profile of v1, /device:TPU:1, one launch (start us, length us, event | category | flops | bytes accessed | tf_op | source)
XLA Modules:
  0.0 63.8 jit_solution(13214340658488202112)
XLA Ops:
  0.6 0.8 %copy.14 = s32[4,16,3]{2,1,0:T(8,128)S(1)} copy(s32[4,16,3]{1,0,2:T(4,128)} %param.20) | data formatting | bytes 1536 | tf_op args[9]
  1.4 0.1 reshape.16
  1.6 0.6 pad.4.ids_ref
  2.1 58.5 %shard_map.122 = (bf16[256,1024]{1,0:T(8,128)(2,1)}, f32[8,1024]{1,0:T(8,128)}) custom-call(s32[1,256]{1,0:T(1,128)} %pad.4.ids_ref, s32[8]{0:T(128)} %len_ref.1, bf16[256,1024]{1,0:T(8,128)(2,1)} %tok_ref.1, f32[1,1024]{1,0:T(1,128)} %bitcast.3, f32[1,1024]{1,0:T(1,128)} %bitcast.4, f32[1,1024]{1,0:T(1,128)} %bitcast.5, bf16[1024,1024]{1,0:T(8,128)(2,1)} %wq_hbm.1, ...), custom_call_target="tpu_custom_call" | custom-call | tf_op jit(solution)/shard_map/pallas_call | solution.py:367
  60.6 1.9 %copy.17 = bf16[256,1024]{1,0:T(8,128)(2,1)} copy(bf16[256,1024]{1,0:T(8,128)(2,1)} %get-tuple-element.4) | data formatting | bytes 1048576
  62.5 1.4 %copy.18 = f32[8,1024]{1,0:T(8,128)} copy(f32[8,1024]{1,0:T(8,128)} %get-tuple-element.5) | data formatting | bytes 65536

commit v2 on v1

v2 whole, which is shorter than its diff:
```python
import jax
import jax.numpy as jnp
from jax import lax
from jax.experimental import pallas as pl
from jax.experimental.pallas import tpu as pltpu
from jax.sharding import PartitionSpec as P

HEADS = 16
BLK = 64
RAND = 3
DOCS = 8
D = 1024
ROWS = 256
SEQ = 8192
NBLK = 128
SIDE = 4
CHIPS = 16
SHARDS = 32
IDS = HEADS * RAND * (ROWS // BLK)
QROWS = 144
KEYS = 6 * BLK

MESH = pl.DeviceIdType.MESH
BF = jnp.bfloat16
F32 = jnp.float32
MASKED = -240000.0
EXP_SCALE = 0.125 * 1.4426950408889634


ORDER = (0, 1, 3, 2)
STEP = 4
GROUPS = CHIPS // STEP


def turn(a):
    return a + lax.div(a, 2) * (1 - 2 * lax.rem(a, 2))


def kernel(
    ids_ref, len_ref, tok_hbm, gain_ref, bias_ref, pbias_ref,
    wq_hbm, wk_hbm, wv_hbm, wo_hbm, wp_hbm,
    enc_ref, doc_ref,
    tok_ref, wq, wk, wv, wo, wp,
    kv_send, kv_buf, q_send, q_recv, att_send, att_recv, doc_send, doc_recv,
    ids_recv, ids_smem, masks, scores, weights, inverse, lhs, mixed,
    w_sem, own_sem, ids_ss, ids_rs, kv_ss, kv_rs, sib_ss, sib_rs,
    q_ss, q_rs, att_ss, att_rs, doc_ss, doc_rs,
):
    dp = lax.axis_index("dp")
    me = lax.axis_index("ctx")
    core = lax.rem(me, 2)
    chip = lax.div(me, 2)
    cx = lax.div(chip, SIDE)
    cz = lax.rem(chip, SIDE)

    ahead_x = [lax.rem(cx + d, SIDE) for d in ORDER]
    ahead_z = [lax.rem(cz + d, SIDE) for d in ORDER]
    back_x = [lax.rem(cx + SIDE - d, SIDE) for d in ORDER]
    back_z = [lax.rem(cz + SIDE - d, SIDE) for d in ORDER]
    ahead = [x * SIDE + z for x in ahead_x for z in ahead_z]
    back = [x * SIDE + z for x in back_x for z in back_z]

    def to_ctx(c):
        return (dp, 2 * c + core)

    sibling = (dp, 2 * chip + 1 - core)

    barrier = pltpu.get_barrier_semaphore()

    def greet(j, carry):
        pl.semaphore_signal(
            barrier, inc=1, device_id=(dp, lax.rem(me + j, SHARDS)), device_id_type=MESH
        )
        return carry

    def tok_load():
        return pltpu.make_async_copy(tok_hbm, tok_ref, own_sem.at[0])

    def kv_load(g, n):
        cols = pl.ds(pl.multiple_of(g * 256, 256), 256)
        src, dst = ((wk_hbm, wk), (wv_hbm, wv))[n]
        return pltpu.make_async_copy(src.at[:, cols], dst.at[:, cols], w_sem.at[2 * g + n])

    def late_load(n):
        src, dst = ((wq_hbm, wq), (wo_hbm, wo), (wp_hbm, wp))[n]
        return pltpu.make_async_copy(src, dst, w_sem.at[8 + n])

    tok_load().start()
    for g in range(4):
        for n in range(2):
            kv_load(g, n).start()
    for n in range(3):
        late_load(n).start()
    lax.fori_loop(1, SHARDS, greet, 0)

    lane = lax.broadcasted_iota(jnp.int32, (1, 128), 1)
    low = lane < 64

    def interleave(first, second):
        return (
            jnp.where(low, first, pltpu.roll(second, 64, 1)),
            jnp.where(low, pltpu.roll(first, 64, 1), second),
        )

    ends, starts = [], []
    total = jnp.int32(0)
    for d in range(DOCS):
        starts.append(total)
        total = total + len_ref[d]
        ends.append(total)

    def rows_of(i):
        return pl.ds(4 * i + 1, 4)

    tok_load().wait()

    def kv_step(g, carry):
        kv_load(g, 0).wait()
        kv_load(g, 1).wait()
        cols = pl.ds(pl.multiple_of(g * 256, 256), 256)
        k = jnp.dot(tok_ref[...], wk[:, cols], preferred_element_type=F32)
        v = jnp.dot(tok_ref[...], wv[:, cols], preferred_element_type=F32)
        for p in range(2):
            s = slice(128 * p, 128 * p + 128)
            even, odd = interleave(k[:, s], v[:, s])
            kv_send[4 * g + 2 * p] = even.astype(BF).reshape(4, BLK, 128)
            kv_send[4 * g + 2 * p + 1] = odd.astype(BF).reshape(4, BLK, 128)
        return carry

    lax.fori_loop(0, 4, kv_step, 0)

    pl.semaphore_wait(barrier, SHARDS - 1)

    def remote(src, dst, send_sem, recv_sem, device):
        return pltpu.make_async_remote_copy(
            src_ref=src, dst_ref=dst, send_sem=send_sem, recv_sem=recv_sem,
            device_id=device, device_id_type=MESH,
        )

    def ids_copy(k):
        return remote(ids_ref, ids_recv.at[chip], ids_ss, ids_rs, to_ctx(ahead[k]))

    def kv_copy(k):
        return remote(
            kv_send.at[ahead[k]], kv_buf.at[rows_of(me)], kv_ss, kv_rs.at[k], to_ctx(ahead[k])
        )

    def q_copy(k):
        return remote(
            q_send.at[ahead[k]], q_recv.at[k], q_ss, q_rs.at[k // STEP], to_ctx(ahead[k])
        )

    def sib_copy(k):
        rows = rows_of(2 * back[k] + core)
        src = kv_send.at[chip] if k == 0 else kv_buf.at[rows]
        return remote(src, kv_buf.at[rows], sib_ss, sib_rs, sibling)

    def doc_copy(j):
        return remote(doc_send, doc_recv.at[me], doc_ss, doc_rs, (dp, lax.rem(me + j, SHARDS)))

    def drain(ref, sem):
        pltpu.make_async_copy(ref, ref, sem).wait()

    for k in range(1, CHIPS):
        kv_copy(k).start()
    sib_copy(0).start()
    pltpu.make_async_copy(kv_send.at[chip], kv_buf.at[rows_of(me)], own_sem.at[1]).start()

    first_row = me * ROWS
    pick_row = lax.broadcasted_iota(jnp.int32, (16, 1), 0)
    pick = jnp.full((16, 1), -1, jnp.int32)
    for d in range(DOCS):
        pick = jnp.where(pick_row == d, starts[d], pick)
    pos = first_row + lax.broadcasted_iota(jnp.int32, (1, ROWS), 1)
    chooser = jnp.where(pick == pos, 1.0, 0.0).astype(BF)

    late_load(0).wait()

    def q_step(g, carry):
        cols = pl.ds(pl.multiple_of(g * 256, 256), 256)
        q = jnp.dot(tok_ref[...], wq[:, cols], preferred_element_type=F32)
        t = jnp.dot(chooser, tok_ref[:, cols], preferred_element_type=F32)
        for p in range(2):
            s = slice(128 * p, 128 * p + 128)
            even, odd = interleave(q[:128, s], q[128:, s])
            q_send[4 * g + 2 * p, 0:128, :] = even.astype(BF)
            q_send[4 * g + 2 * p + 1, 0:128, :] = odd.astype(BF)
            q_send[4 * g + 2 * p, 128:QROWS, :] = t[:, s].astype(BF)
            q_send[4 * g + 2 * p + 1, 128:QROWS, :] = pltpu.roll(t[:, s], 64, 1).astype(BF)
        return carry

    lax.fori_loop(0, 4, q_step, 0)
    for k in range(1, CHIPS):
        ids_copy(k).start()
    pltpu.make_async_copy(ids_ref, ids_recv.at[chip], ids_rs).start()
    for k in range(1, CHIPS):
        q_copy(k).start()
    pltpu.make_async_copy(q_send.at[chip], q_recv.at[0], q_rs.at[0]).start()

    kv_buf[0] = jnp.zeros((BLK, 128), BF)
    kv_buf[NBLK + 1] = jnp.zeros((BLK, 128), BF)

    col = lax.broadcasted_iota(jnp.int32, (1, 256), 1)
    diagonal = (
        lax.broadcasted_iota(jnp.int32, (BLK, 128), 1)
        == lax.broadcasted_iota(jnp.int32, (BLK, 128), 0) + BLK
    )

    def make_masks(k):
        first = (2 * back[k] + core) * (ROWS // BLK)
        for block in range(4):
            kpos = (first + block - 1) * BLK + col
            kdoc = jnp.zeros((1, 256), F32)
            for d in range(DOCS):
                kdoc = kdoc + jnp.where(kpos >= ends[d], 1.0, 0.0)
            kdoc = jnp.where((kpos < 0) | (kpos >= SEQ), -1.0, kdoc)
            qdoc = jnp.sum(jnp.where(diagonal, kdoc[:, :128], 0.0), axis=1, keepdims=True)
            keep = (qdoc == kdoc) | (col >= 3 * BLK)
            masks[4 * k + block] = jnp.where(keep, 1, 0)

    make_masks(0)
    for k in range(1, CHIPS):
        make_masks(k)
        kv_copy(k).wait_recv()
        sib_copy(k).start()
    drain(ids_recv, ids_rs)
    to_smem = pltpu.make_async_copy(ids_recv, ids_smem, own_sem.at[3])
    to_smem.start()
    to_smem.wait()
    drain(kv_send.at[0], own_sem.at[1])
    drain(kv_send, sib_rs)

    def attend(g, carry):
        drain(q_recv.at[pl.ds(0, STEP)], q_rs.at[g])
        homes = []
        for i in range(STEP):
            k = g * STEP + i
            dx, dz = turn(lax.div(k, SIDE)), turn(lax.rem(k, SIDE))
            x = lax.rem(cx + SIDE - dx, SIDE)
            homes.append(x * SIDE + lax.rem(cz + SIDE - dz, SIDE))

        def keys_of(i, block):
            c = homes[i]
            b = (2 * c + core) * (ROWS // BLK) + block
            parts = [kv_buf[pl.ds(b, 3)].reshape(3 * BLK, 128)]
            for r in range(RAND):
                at = ids_smem[c, 0, block * HEADS * RAND + chip * RAND + r]
                parts.append(kv_buf[at + 1])
            return jnp.concatenate(parts, axis=0)

        def score(i):
            for j in range(2):
                pair = q_recv[g * STEP + i, BLK * j:BLK * j + BLK, :].astype(F32)
                for half in range(2):
                    block = j + 2 * half
                    q = pltpu.roll(pair, 64, 1) if half else pair
                    q = jnp.where(low, q, 0.0).astype(BF)
                    scores[4 * i + block] = lax.dot_general(
                        q, keys_of(i, block), (((1,), (1,)), ((), ())),
                        preferred_element_type=F32,
                    )

        def soften(i):
            for block in range(4):
                t = 4 * i + block
                keep = masks[4 * (g * STEP + i) + block] > 0
                s0 = jnp.where(keep, scores[t, :, 0:256], MASKED)
                s1 = scores[t, :, 256:KEYS]
                m = jnp.maximum(jnp.maximum(s0[:, :128], s0[:, 128:]), s1)
                m = jnp.max(m, axis=1, keepdims=True)
                w0 = jnp.exp2((s0 - m) * EXP_SCALE)
                w1 = jnp.exp2((s1 - m) * EXP_SCALE)
                weights[t, :, 0:256] = w0.astype(BF)
                weights[t, :, 256:KEYS] = w1.astype(BF)
                l = jnp.sum(w0[:, :128] + w0[:, 128:] + w1, axis=1, keepdims=True)
                inverse[t] = jnp.broadcast_to(1.0 / l, (BLK, 128))

        def gather(i):
            for j in range(2):
                outs = []
                for half in range(2):
                    t = 4 * i + j + 2 * half
                    o = jnp.dot(
                        weights[t], keys_of(i, j + 2 * half), preferred_element_type=F32
                    )
                    outs.append(o * inverse[t])
                att_send[homes[i], 4 * j:4 * j + 4] = jnp.where(
                    low, pltpu.roll(outs[0], 64, 1), outs[1]
                ).astype(BF).reshape(4, 16, 128)

        for i in range(STEP + 2):
            if i < STEP:
                score(i)
            if 1 <= i <= STEP:
                soften(i - 1)
            if i >= 2:
                gather(i - 2)

        for i in range(STEP):
            c = homes[i]

            def send(c=c):
                remote(
                    att_send.at[c], att_recv.at[chip], att_ss, att_rs.at[g], to_ctx(c)
                ).start()

            if i == 0:
                pl.when(g > 0)(send)
            else:
                send()
        return carry

    lax.fori_loop(0, GROUPS, attend, 0)
    pltpu.make_async_copy(att_send.at[chip], att_recv.at[chip], att_rs.at[0]).start()

    tok_piece = jnp.zeros((16, 128), F32)
    for k in range(CHIPS):
        tok_piece = tok_piece + q_recv[k, 128:QROWS, :].astype(F32)
    att_piece = jnp.zeros((8, 128), F32)
    row8 = lax.broadcasted_iota(jnp.int32, (8, 1), 0)
    row16 = lax.broadcasted_iota(jnp.int32, (16, 1), 0)
    for d in range(DOCS):
        home = lax.div(starts[d], ROWS)
        local = lax.rem(starts[d], ROWS)
        packed = lax.rem(local, 128)
        tile = att_send[lax.div(home, 2), lax.div(packed, 16)].astype(F32)
        here = row16 + 16 * core == lax.rem(packed, 16) + 16 * lax.rem(home, 2)
        one = jnp.where(here, tile, 0.0)
        one = jnp.sum(one, axis=0, keepdims=True)
        one = jnp.where(lane * 0 + local >= 128, pltpu.roll(one, 64, 1), one)
        att_piece = jnp.where(row8 == d, one, att_piece)
    doc_send[...] = jnp.concatenate((att_piece, tok_piece[:8]), axis=0).astype(BF)
    for j in range(1, SHARDS):
        doc_copy(j).start()
    pltpu.make_async_copy(doc_send, doc_recv.at[me], doc_rs).start()

    late_load(1).wait()
    for g in range(4):
        drain(att_recv.at[pl.ds(0, 4)], att_rs.at[g])
        x = ahead_x[g]
        for p in range(2):
            even = att_recv[4 * x + 2 * p].reshape(128, 128).astype(F32)
            odd = att_recv[4 * x + 2 * p + 1].reshape(128, 128).astype(F32)
            top, bottom = interleave(even, odd)
            s = slice(128 * p, 128 * p + 128)
            lhs[0:128, s] = top.astype(BF)
            lhs[128:256, s] = bottom.astype(BF)
        if g == 3:
            drain(doc_recv, doc_rs)
        heads = pl.ds(pl.multiple_of(x * 256, 256), 256)
        y = jnp.dot(lhs[...], wo[heads, :], preferred_element_type=F32)
        if g == 0:
            mixed[...] = tok_ref[...].astype(F32) + y
        else:
            mixed[...] = mixed[...] + y

    pieces = [
        doc_recv[2 * h].astype(F32) + doc_recv[2 * h + 1].astype(F32) for h in range(CHIPS)
    ]
    opened = jnp.concatenate(
        [
            jnp.where(low, pieces[2 * j], pltpu.roll(pieces[2 * j + 1], 64, 1))
            for j in range(CHIPS // 2)
        ],
        axis=1,
    )
    y = jnp.dot(opened.astype(BF), wo[...], preferred_element_type=F32)
    opened_mixed = opened[8:] + y[:8]

    def normed(rows):
        centre = jnp.mean(rows, axis=1, keepdims=True)
        spread = jnp.mean(jnp.square(rows - centre), axis=1, keepdims=True)
        return ((rows - centre) * lax.rsqrt(spread + 1e-05) * gain_ref[...] + bias_ref[...]).astype(BF)

    def norm_step(n, carry):
        rows = pl.ds(pl.multiple_of(n * 64, 64), 64)
        enc_ref[rows, :] = normed(mixed[rows, :])
        return carry

    lax.fori_loop(0, 4, norm_step, 0)
    late_load(2).wait()
    doc_ref[...] = jnp.tanh(
        jnp.dot(normed(opened_mixed), wp[...], preferred_element_type=F32) + pbias_ref[...]
    )

    others = pl.ds(0, CHIPS - 1)
    drain(ids_recv.at[others], ids_ss)
    drain(kv_send.at[others], kv_ss)
    drain(q_send.at[others], q_ss)
    drain(att_send.at[others], att_ss)
    drain(kv_send, sib_ss)
    drain(doc_recv.at[pl.ds(0, SHARDS - 1)], doc_ss)


def per_device(
    tokens, w_query, w_key, w_value, w_out, norm_gain, norm_bias, w_pool, pool_bias,
    random_ids, lengths,
):
    vmem = pl.BlockSpec(memory_space=pltpu.VMEM)
    smem = pl.BlockSpec(memory_space=pltpu.SMEM)
    hbm = pl.BlockSpec(memory_space=pl.ANY)
    ids = jnp.pad(random_ids.reshape(1, IDS), ((0, 0), (0, 256 - IDS)))
    dma = pltpu.SemaphoreType.DMA
    return pl.pallas_call(
        kernel,
        out_shape=(
            jax.ShapeDtypeStruct((ROWS, D), BF),
            jax.ShapeDtypeStruct((DOCS, D), F32),
        ),
        in_specs=[vmem, smem, hbm, vmem, vmem, vmem, hbm, hbm, hbm, hbm, hbm],
        out_specs=(vmem, vmem),
        scratch_shapes=[
            pltpu.VMEM((ROWS, D), BF),
            pltpu.VMEM((D, D), BF), pltpu.VMEM((D, D), BF), pltpu.VMEM((D, D), BF),
            pltpu.VMEM((D, D), BF), pltpu.VMEM((D, D), BF),
            pltpu.VMEM((CHIPS, 4, BLK, 128), BF),
            pltpu.VMEM((NBLK + 2, BLK, 128), BF),
            pltpu.VMEM((CHIPS, QROWS, 128), BF),
            pltpu.VMEM((CHIPS, QROWS, 128), BF),
            pltpu.VMEM((CHIPS, 8, 16, 128), BF),
            pltpu.VMEM((CHIPS, 8, 16, 128), BF),
            pltpu.VMEM((16, 128), BF),
            pltpu.VMEM((SHARDS, 16, 128), BF),
            pltpu.VMEM((CHIPS, 1, 256), jnp.int32),
            pltpu.SMEM((CHIPS, 1, 256), jnp.int32),
            pltpu.VMEM((CHIPS * 4, BLK, 256), jnp.int32),
            pltpu.VMEM((4 * STEP, BLK, KEYS), F32),
            pltpu.VMEM((4 * STEP, BLK, KEYS), BF),
            pltpu.VMEM((4 * STEP, BLK, 128), F32),
            pltpu.VMEM((ROWS, 256), BF),
            pltpu.VMEM((ROWS, D), F32),
            dma((11,)), dma((4,)), dma, dma, dma, dma((CHIPS,)), dma, dma,
            dma, dma((GROUPS,)), dma, dma((GROUPS,)), dma, dma,
        ],
        compiler_params=pltpu.CompilerParams(
            collective_id=0, has_side_effects=True, vmem_limit_bytes=56 << 20
        ),
    )(
        ids, lengths, tokens, norm_gain.reshape(1, D), norm_bias.reshape(1, D),
        pool_bias.reshape(1, D), w_query, w_key, w_value, w_out, w_pool,
    )


def solution(mesh):
    rows = P(("dp", "ctx"), None)
    placed = (
        rows, P(), P(), P(), P(), P(), P(), P(), P(),
        P(("dp", "ctx"), None, None), P("dp"),
    )
    return jax.shard_map(
        per_device,
        mesh=mesh,
        in_specs=placed,
        out_specs=(rows, P("dp", None)),
        check_vma=False,
    )
```

time: 64.1 us -> 52.6 us (0.82)
  Pallas kernels: 58.5 us -> 46.9 us
    pallas_call x1, Pallas kernels: 58.5 us -> 46.9 us  [per_device(): pl.pallas_call(kernel, out_shape=(jax.ShapeDtypeStruct((ROWS, D), BF), ja...]
where the time goes in v2:
time: 52.6 us; the launch traced here: 52.3 us
  Pallas kernels  46.9 us (89%)
  local copies, waits for them, and re-layouts  4.74 us (9%)
  between operations  0.64 us (1%)
    pallas_call x1, Pallas kernels, per_device(): pl.pallas_call(kernel, out_shape=(jax.ShapeDtypeStruct((ROWS, D), BF), ja...  46.9 us
    unnamed x3, local copies, waits for them, and re-layouts  4.03 us

profile of v2, /device:TPU:1, one launch (start us, length us, event | category | flops | bytes accessed | tf_op | source)
XLA Modules:
  0.0 52.3 jit_solution(12163984657254225155)
XLA Ops:
  0.6 0.8 %copy.14 = s32[4,16,3]{2,1,0:T(8,128)S(1)} copy(s32[4,16,3]{1,0,2:T(4,128)} %param.20) | data formatting | bytes 1536 | tf_op args[9]
  1.4 0.1 reshape.16
  1.6 0.6 %pad.4.ids_ref = s32[1,256]{1,0:T(1,128)} pad(s32[1,192]{1,0:T(1,128)S(1)} %reshape.16, s32[]{:T(128)} %constant.0.clone.1), padding=0_0x0_64 | pad | bytes 1796 | tf_op jit(solution)/shard_map/jit(_pad)/pad | solution.py:402
  2.1 46.9 %shard_map.122 = (bf16[256,1024]{1,0:T(8,128)(2,1)}, f32[8,1024]{1,0:T(8,128)}) custom-call(s32[1,256]{1,0:T(1,128)} %pad.4.ids_ref, s32[8]{0:T(128)} %len_ref.1, bf16[256,1024]{1,0:T(8,128)(2,1)} %tok_hbm.1, f32[1,1024]{1,0:T(1,128)} %bitcast.3, f32[1,1024]{1,0:T(1,128)} %bitcast.4, f32[1,1024]{1,0:T(1,128)} %bitcast.5, bf16[1024,1024]{1,0:T(8,128)(2,1)} %wq_hbm.1, ...), custom_call_target="tpu_custom_call" | custom-call | tf_op jit(solution)/shard_map/pallas_call | solution.py:404
  49.0 1.9 %copy.17 = bf16[256,1024]{1,0:T(8,128)(2,1)} copy(bf16[256,1024]{1,0:T(8,128)(2,1)} %get-tuple-element.4) | data formatting | bytes 1048576
  50.9 1.4 %copy.18 = f32[8,1024]{1,0:T(8,128)} copy(f32[8,1024]{1,0:T(8,128)} %get-tuple-element.5) | data formatting | bytes 65536

commit v3 on v2

--- a/solution.py
+++ b/solution.py
@@ -16,7 +16,6 @@
 SIDE = 4
 CHIPS = 16
 SHARDS = 32
-IDS = HEADS * RAND * (ROWS // BLK)
 QROWS = 144
 KEYS = 6 * BLK
 
@@ -37,10 +36,10 @@
 
 
 def kernel(
-    ids_ref, len_ref, tok_hbm, gain_ref, bias_ref, pbias_ref,
+    ids_hbm, len_hbm, tok_hbm, gain_hbm, bias_hbm, pbias_hbm,
     wq_hbm, wk_hbm, wv_hbm, wo_hbm, wp_hbm,
     enc_ref, doc_ref,
-    tok_ref, wq, wk, wv, wo, wp,
+    ids_ref, len_ref, tok_ref, gain_ref, bias_ref, pbias_ref, wq, wk, wv, wo, wp,
     kv_send, kv_buf, q_send, q_recv, att_send, att_recv, doc_send, doc_recv,
     ids_recv, ids_smem, masks, scores, weights, inverse, lhs, mixed,
     w_sem, own_sem, ids_ss, ids_rs, kv_ss, kv_rs, sib_ss, sib_rs,
@@ -85,10 +84,19 @@
         src, dst = ((wq_hbm, wq), (wo_hbm, wo), (wp_hbm, wp))[n]
         return pltpu.make_async_copy(src, dst, w_sem.at[8 + n])
 
+    def small_load(n):
+        src, dst = (
+            (len_hbm, len_ref), (ids_hbm, ids_ref), (gain_hbm, gain_ref),
+            (bias_hbm, bias_ref), (pbias_hbm, pbias_ref),
+        )[n]
+        return pltpu.make_async_copy(src, dst, own_sem.at[4 + n])
+
     tok_load().start()
     for g in range(4):
         for n in range(2):
             kv_load(g, n).start()
+    for n in range(5):
+        small_load(n).start()
     for n in range(3):
         late_load(n).start()
     lax.fori_loop(1, SHARDS, greet, 0)
@@ -101,13 +109,6 @@
             jnp.where(low, first, pltpu.roll(second, 64, 1)),
             jnp.where(low, pltpu.roll(first, 64, 1), second),
         )
-
-    ends, starts = [], []
-    total = jnp.int32(0)
-    for d in range(DOCS):
-        starts.append(total)
-        total = total + len_ref[d]
-        ends.append(total)
 
     def rows_of(i):
         return pl.ds(4 * i + 1, 4)
@@ -166,6 +167,14 @@
     sib_copy(0).start()
     pltpu.make_async_copy(kv_send.at[chip], kv_buf.at[rows_of(me)], own_sem.at[1]).start()
 
+    small_load(0).wait()
+    ends, starts = [], []
+    total = jnp.int32(0)
+    for d in range(DOCS):
+        starts.append(total)
+        total = total + len_ref[d]
+        ends.append(total)
+
     first_row = me * ROWS
     pick_row = lax.broadcasted_iota(jnp.int32, (16, 1), 0)
     pick = jnp.full((16, 1), -1, jnp.int32)
@@ -190,6 +199,7 @@
         return carry
 
     lax.fori_loop(0, 4, q_step, 0)
+    small_load(1).wait()
     for k in range(1, CHIPS):
         ids_copy(k).start()
     pltpu.make_async_copy(ids_ref, ids_recv.at[chip], ids_rs).start()
@@ -244,7 +254,7 @@
             b = (2 * c + core) * (ROWS // BLK) + block
             parts = [kv_buf[pl.ds(b, 3)].reshape(3 * BLK, 128)]
             for r in range(RAND):
-                at = ids_smem[c, 0, block * HEADS * RAND + chip * RAND + r]
+                at = ids_smem[c, r, block, chip]
                 parts.append(kv_buf[at + 1])
             return jnp.concatenate(parts, axis=0)
 
@@ -372,6 +382,9 @@
         spread = jnp.mean(jnp.square(rows - centre), axis=1, keepdims=True)
         return ((rows - centre) * lax.rsqrt(spread + 1e-05) * gain_ref[...] + bias_ref[...]).astype(BF)
 
+    for n in range(2, 5):
+        small_load(n).wait()
+
     def norm_step(n, carry):
         rows = pl.ds(pl.multiple_of(n * 64, 64), 64)
         enc_ref[rows, :] = normed(mixed[rows, :])
@@ -397,9 +410,8 @@
     random_ids, lengths,
 ):
     vmem = pl.BlockSpec(memory_space=pltpu.VMEM)
-    smem = pl.BlockSpec(memory_space=pltpu.SMEM)
-    hbm = pl.BlockSpec(memory_space=pl.ANY)
-    ids = jnp.pad(random_ids.reshape(1, IDS), ((0, 0), (0, 256 - IDS)))
+    hbm = pl.BlockSpec(memory_space=pltpu.HBM)
+    ids = random_ids.transpose(2, 0, 1)
     dma = pltpu.SemaphoreType.DMA
     return pl.pallas_call(
         kernel,
@@ -407,10 +419,12 @@
             jax.ShapeDtypeStruct((ROWS, D), BF),
             jax.ShapeDtypeStruct((DOCS, D), F32),
         ),
-        in_specs=[vmem, smem, hbm, vmem, vmem, vmem, hbm, hbm, hbm, hbm, hbm],
+        in_specs=[hbm] * 11,
         out_specs=(vmem, vmem),
         scratch_shapes=[
+            pltpu.VMEM((RAND, 4, HEADS), jnp.int32), pltpu.SMEM((DOCS,), jnp.int32),
             pltpu.VMEM((ROWS, D), BF),
+            pltpu.VMEM((1, D), F32), pltpu.VMEM((1, D), F32), pltpu.VMEM((1, D), F32),
             pltpu.VMEM((D, D), BF), pltpu.VMEM((D, D), BF), pltpu.VMEM((D, D), BF),
             pltpu.VMEM((D, D), BF), pltpu.VMEM((D, D), BF),
             pltpu.VMEM((CHIPS, 4, BLK, 128), BF),
@@ -421,24 +435,27 @@
             pltpu.VMEM((CHIPS, 8, 16, 128), BF),
             pltpu.VMEM((16, 128), BF),
             pltpu.VMEM((SHARDS, 16, 128), BF),
-            pltpu.VMEM((CHIPS, 1, 256), jnp.int32),
-            pltpu.SMEM((CHIPS, 1, 256), jnp.int32),
+            pltpu.VMEM((CHIPS, RAND, 4, HEADS), jnp.int32),
+            pltpu.SMEM((CHIPS, RAND, 4, HEADS), jnp.int32),
             pltpu.VMEM((CHIPS * 4, BLK, 256), jnp.int32),
             pltpu.VMEM((4 * STEP, BLK, KEYS), F32),
             pltpu.VMEM((4 * STEP, BLK, KEYS), BF),
             pltpu.VMEM((4 * STEP, BLK, 128), F32),
             pltpu.VMEM((ROWS, 256), BF),
             pltpu.VMEM((ROWS, D), F32),
-            dma((11,)), dma((4,)), dma, dma, dma, dma((CHIPS,)), dma, dma,
+            dma((11,)), dma((9,)), dma, dma, dma, dma((CHIPS,)), dma, dma,
             dma, dma((GROUPS,)), dma, dma((GROUPS,)), dma, dma,
         ],
         compiler_params=pltpu.CompilerParams(
-            collective_id=0, has_side_effects=True, vmem_limit_bytes=56 << 20
+            collective_id=0, has_side_effects=True, vmem_limit_bytes=32 << 20
         ),
-    )(
-        ids, lengths, tokens, norm_gain.reshape(1, D), norm_bias.reshape(1, D),
-        pool_bias.reshape(1, D), w_query, w_key, w_value, w_out, w_pool,
-    )
+    )(*[
+        pltpu.with_memory_space_constraint(x, pltpu.HBM)
+        for x in (
+            ids, lengths, tokens, norm_gain.reshape(1, D), norm_bias.reshape(1, D),
+            pool_bias.reshape(1, D), w_query, w_key, w_value, w_out, w_pool,
+        )
+    ])
 
 
 def solution(mesh):

time: 52.6 us -> 46.7 us (0.89)
  local copies, waits for them, and re-layouts: 4.74 us -> 1.41 us
  Pallas kernels: 46.9 us -> 44.5 us
    unnamed x3 -> x2, local copies, waits for them, and re-layouts: 4.03 us -> 1.41 us
    pallas_call x1, Pallas kernels: 46.9 us -> 44.5 us  [per_device(): pl.pallas_call(kernel, out_shape=(jax.ShapeDtypeStruct((ROWS, D), BF), ja...]
    pad x1 -> x0, local copies, waits for them, and re-layouts: 0.57 us -> none  [per_device(): ids = jnp.pad(random_ids.reshape(1, IDS), ((0, 0), (0, 256 - IDS)))]
where the time goes in v3:
time: 46.7 us; the launch traced here: 46.6 us
  Pallas kernels  44.5 us (95%)
  local copies, waits for them, and re-layouts  1.41 us (3%)
  between operations  0.64 us (1%)
    pallas_call x1, Pallas kernels, per_device(): pl.pallas_call(kernel, out_shape=(jax.ShapeDtypeStruct((ROWS, D), BF), ja...  44.5 us
    unnamed x2, local copies, waits for them, and re-layouts  1.41 us

profile of v3, /device:TPU:1, one launch (start us, length us, event | category | flops | bytes accessed | tf_op | source)
XLA Modules:
  0.0 46.6 jit_solution(8920569461486741349)
XLA Ops:
  0.6 44.5 %shard_map.122 = (bf16[256,1024]{1,0:T(8,128)(2,1)S(1)}, f32[8,1024]{1,0:T(8,128)S(1)}) custom-call(s32[3,4,16]{2,1,0:T(4,128)} %bitcast.4, s32[8]{0:T(128)} %len_hbm.1, bf16[256,1024]{1,0:T(8,128)(2,1)} %tok_hbm.1, f32[1,1024]{1,0:T(1,128)} %bitcast.5, f32[1,1024]{1,0:T(1,128)} %bitcast.6, f32[1,1024]{1,0:T(1,128)} %bitcast.7, bf16[1024,1024]{1,0:T(8,128)(2,1)} %wq_hbm.1, ...), custom_call_target="tpu_custom_call" | custom-call | tf_op jit(solution)/shard_map/pallas_call | solution.py:416
  45.2 0.8 %copy.15 = bf16[256,1024]{1,0:T(8,128)(2,1)} copy(bf16[256,1024]{1,0:T(8,128)(2,1)S(1)} %get-tuple-element.4) | data formatting | bytes 1048576
  46.0 0.6 %copy.16 = f32[8,1024]{1,0:T(8,128)} copy(f32[8,1024]{1,0:T(8,128)S(1)} %get-tuple-element.5) | data formatting | bytes 65536

commit v4 on v3

--- a/solution.py
+++ b/solution.py
@@ -16,7 +16,7 @@
 SIDE = 4
 CHIPS = 16
 SHARDS = 32
-QROWS = 144
+QROWS = 136
 KEYS = 6 * BLK
 
 MESH = pl.DeviceIdType.MESH
@@ -26,13 +26,11 @@
 EXP_SCALE = 0.125 * 1.4426950408889634
 
 
-ORDER = (0, 1, 3, 2)
+ORDER_X = (3, 2, 1, 0)
+ORDER_Z = (0, 1, 3, 2)
+OWN = 12
 STEP = 4
 GROUPS = CHIPS // STEP
-
-
-def turn(a):
-    return a + lax.div(a, 2) * (1 - 2 * lax.rem(a, 2))
 
 
 def kernel(
@@ -40,10 +38,10 @@
     wq_hbm, wk_hbm, wv_hbm, wo_hbm, wp_hbm,
     enc_ref, doc_ref,
     ids_ref, len_ref, tok_ref, gain_ref, bias_ref, pbias_ref, wq, wk, wv, wo, wp,
-    kv_send, kv_buf, q_send, q_recv, att_send, att_recv, doc_send, doc_recv,
-    ids_recv, ids_smem, masks, scores, weights, inverse, lhs, mixed,
+    kv_send, kv_buf, q_send, q_recv, att_send, att_recv, doc_send, doc_near, doc_sum, doc_recv,
+    ids_row, ids_recv, ids_smem, masks, scores, weights, inverse, lhs, mixed,
     w_sem, own_sem, ids_ss, ids_rs, kv_ss, kv_rs, sib_ss, sib_rs,
-    q_ss, q_rs, att_ss, att_rs, doc_ss, doc_rs,
+    q_ss, q_rs, att_ss, att_rs, near_ss, near_rs, doc_ss, doc_rs,
 ):
     dp = lax.axis_index("dp")
     me = lax.axis_index("ctx")
@@ -52,10 +50,11 @@
     cx = lax.div(chip, SIDE)
     cz = lax.rem(chip, SIDE)
 
-    ahead_x = [lax.rem(cx + d, SIDE) for d in ORDER]
-    ahead_z = [lax.rem(cz + d, SIDE) for d in ORDER]
-    back_x = [lax.rem(cx + SIDE - d, SIDE) for d in ORDER]
-    back_z = [lax.rem(cz + SIDE - d, SIDE) for d in ORDER]
+    ahead_x = [lax.rem(cx + d, SIDE) for d in ORDER_X]
+    ahead_z = [lax.rem(cz + d, SIDE) for d in ORDER_Z]
+    back_x = [lax.rem(cx + SIDE - d, SIDE) for d in ORDER_X]
+    back_z = [lax.rem(cz + SIDE - d, SIDE) for d in ORDER_Z]
+    others = [k for k in range(CHIPS) if k != OWN]
     ahead = [x * SIDE + z for x in ahead_x for z in ahead_z]
     back = [x * SIDE + z for x in back_x for z in back_z]
 
@@ -66,11 +65,8 @@
 
     barrier = pltpu.get_barrier_semaphore()
 
-    def greet(j, carry):
-        pl.semaphore_signal(
-            barrier, inc=1, device_id=(dp, lax.rem(me + j, SHARDS)), device_id_type=MESH
-        )
-        return carry
+    def greet(device):
+        pl.semaphore_signal(barrier, inc=1, device_id=device, device_id_type=MESH)
 
     def tok_load():
         return pltpu.make_async_copy(tok_hbm, tok_ref, own_sem.at[0])
@@ -91,6 +87,9 @@
         )[n]
         return pltpu.make_async_copy(src, dst, own_sem.at[4 + n])
 
+    for k in others:
+        greet(to_ctx(ahead[k]))
+    greet(sibling)
     tok_load().start()
     for g in range(4):
         for n in range(2):
@@ -99,7 +98,6 @@
         small_load(n).start()
     for n in range(3):
         late_load(n).start()
-    lax.fori_loop(1, SHARDS, greet, 0)
 
     lane = lax.broadcasted_iota(jnp.int32, (1, 128), 1)
     low = lane < 64
@@ -130,7 +128,12 @@
 
     lax.fori_loop(0, 4, kv_step, 0)
 
-    pl.semaphore_wait(barrier, SHARDS - 1)
+    small_load(1).wait()
+    row_ids = [ids_ref[r, b:b + 1, :] for r in range(RAND) for b in range(4)]
+    ids_row[:, 0:128] = jnp.concatenate(row_ids[:8], axis=1)
+    ids_row[:, 128:256] = jnp.concatenate(row_ids[8:] + row_ids[8:], axis=1)
+
+    pl.semaphore_wait(barrier, CHIPS)
 
     def remote(src, dst, send_sem, recv_sem, device):
         return pltpu.make_async_remote_copy(
@@ -139,7 +142,7 @@
         )
 
     def ids_copy(k):
-        return remote(ids_ref, ids_recv.at[chip], ids_ss, ids_rs, to_ctx(ahead[k]))
+        return remote(ids_row, ids_recv.at[chip], ids_ss, ids_rs, to_ctx(ahead[k]))
 
     def kv_copy(k):
         return remote(
@@ -153,18 +156,21 @@
 
     def sib_copy(k):
         rows = rows_of(2 * back[k] + core)
-        src = kv_send.at[chip] if k == 0 else kv_buf.at[rows]
+        src = kv_send.at[chip] if k == OWN else kv_buf.at[rows]
         return remote(src, kv_buf.at[rows], sib_ss, sib_rs, sibling)
 
     def doc_copy(j):
-        return remote(doc_send, doc_recv.at[me], doc_ss, doc_rs, (dp, lax.rem(me + j, SHARDS)))
+        return remote(doc_sum, doc_recv.at[chip], doc_ss, doc_rs, to_ctx(ahead[j]))
 
     def drain(ref, sem):
         pltpu.make_async_copy(ref, ref, sem).wait()
 
-    for k in range(1, CHIPS):
+    for k in others:
+        ids_copy(k).start()
+    for k in others:
         kv_copy(k).start()
-    sib_copy(0).start()
+    pltpu.make_async_copy(ids_row, ids_recv.at[chip], ids_rs).start()
+    sib_copy(OWN).start()
     pltpu.make_async_copy(kv_send.at[chip], kv_buf.at[rows_of(me)], own_sem.at[1]).start()
 
     small_load(0).wait()
@@ -176,8 +182,8 @@
         ends.append(total)
 
     first_row = me * ROWS
-    pick_row = lax.broadcasted_iota(jnp.int32, (16, 1), 0)
-    pick = jnp.full((16, 1), -1, jnp.int32)
+    pick_row = lax.broadcasted_iota(jnp.int32, (8, 1), 0)
+    pick = jnp.full((8, 1), -1, jnp.int32)
     for d in range(DOCS):
         pick = jnp.where(pick_row == d, starts[d], pick)
     pos = first_row + lax.broadcasted_iota(jnp.int32, (1, ROWS), 1)
@@ -199,13 +205,9 @@
         return carry
 
     lax.fori_loop(0, 4, q_step, 0)
-    small_load(1).wait()
-    for k in range(1, CHIPS):
-        ids_copy(k).start()
-    pltpu.make_async_copy(ids_ref, ids_recv.at[chip], ids_rs).start()
-    for k in range(1, CHIPS):
+    for k in others:
         q_copy(k).start()
-    pltpu.make_async_copy(q_send.at[chip], q_recv.at[0], q_rs.at[0]).start()
+    pltpu.make_async_copy(q_send.at[chip], q_recv.at[OWN], q_rs.at[OWN // STEP]).start()
 
     kv_buf[0] = jnp.zeros((BLK, 128), BF)
     kv_buf[NBLK + 1] = jnp.zeros((BLK, 128), BF)
@@ -228,14 +230,14 @@
             keep = (qdoc == kdoc) | (col >= 3 * BLK)
             masks[4 * k + block] = jnp.where(keep, 1, 0)
 
-    make_masks(0)
-    for k in range(1, CHIPS):
+    drain(ids_recv, ids_rs)
+    to_smem = pltpu.make_async_copy(ids_recv, ids_smem, own_sem.at[3])
+    to_smem.start()
+    make_masks(OWN)
+    for k in others:
         make_masks(k)
         kv_copy(k).wait_recv()
         sib_copy(k).start()
-    drain(ids_recv, ids_rs)
-    to_smem = pltpu.make_async_copy(ids_recv, ids_smem, own_sem.at[3])
-    to_smem.start()
     to_smem.wait()
     drain(kv_send.at[0], own_sem.at[1])
     drain(kv_send, sib_rs)
@@ -244,17 +246,15 @@
         drain(q_recv.at[pl.ds(0, STEP)], q_rs.at[g])
         homes = []
         for i in range(STEP):
-            k = g * STEP + i
-            dx, dz = turn(lax.div(k, SIDE)), turn(lax.rem(k, SIDE))
-            x = lax.rem(cx + SIDE - dx, SIDE)
-            homes.append(x * SIDE + lax.rem(cz + SIDE - dz, SIDE))
+            x = lax.rem(cx + 1 + g, SIDE)
+            homes.append(x * SIDE + back_z[i])
 
         def keys_of(i, block):
             c = homes[i]
             b = (2 * c + core) * (ROWS // BLK) + block
             parts = [kv_buf[pl.ds(b, 3)].reshape(3 * BLK, 128)]
             for r in range(RAND):
-                at = ids_smem[c, r, block, chip]
+                at = ids_smem[c, 0, (4 * r + block) * HEADS + chip]
                 parts.append(kv_buf[at + 1])
             return jnp.concatenate(parts, axis=0)
 
@@ -298,32 +298,33 @@
                     low, pltpu.roll(outs[0], 64, 1), outs[1]
                 ).astype(BF).reshape(4, 16, 128)
 
-        for i in range(STEP + 2):
-            if i < STEP:
-                score(i)
-            if 1 <= i <= STEP:
-                soften(i - 1)
-            if i >= 2:
-                gather(i - 2)
-
-        for i in range(STEP):
-            c = homes[i]
-
-            def send(c=c):
+        def give_back(i):
+            def send():
                 remote(
-                    att_send.at[c], att_recv.at[chip], att_ss, att_rs.at[g], to_ctx(c)
+                    att_send.at[homes[i]], att_recv.at[chip], att_ss, att_rs.at[g],
+                    to_ctx(homes[i]),
                 ).start()
 
-            if i == 0:
-                pl.when(g > 0)(send)
+            if i == OWN % STEP:
+                pl.when(g != OWN // STEP)(send)
             else:
                 send()
+
+        for i in range(STEP):
+            score(i)
+        for i in range(STEP):
+            soften(i)
+        for i in range(STEP):
+            gather(i)
+        for i in range(STEP):
+            give_back(i)
+
         return carry
 
     lax.fori_loop(0, GROUPS, attend, 0)
-    pltpu.make_async_copy(att_send.at[chip], att_recv.at[chip], att_rs.at[0]).start()
-
-    tok_piece = jnp.zeros((16, 128), F32)
+    pltpu.make_async_copy(att_send.at[chip], att_recv.at[chip], att_rs.at[GROUPS - 1]).start()
+
+    tok_piece = jnp.zeros((8, 128), F32)
     for k in range(CHIPS):
         tok_piece = tok_piece + q_recv[k, 128:QROWS, :].astype(F32)
     att_piece = jnp.zeros((8, 128), F32)
@@ -339,13 +340,40 @@
         one = jnp.sum(one, axis=0, keepdims=True)
         one = jnp.where(lane * 0 + local >= 128, pltpu.roll(one, 64, 1), one)
         att_piece = jnp.where(row8 == d, one, att_piece)
-    doc_send[...] = jnp.concatenate((att_piece, tok_piece[:8]), axis=0).astype(BF)
-    for j in range(1, SHARDS):
-        doc_copy(j).start()
-    pltpu.make_async_copy(doc_send, doc_recv.at[me], doc_rs).start()
+    doc_send[...] = jnp.concatenate((att_piece, tok_piece), axis=0).astype(BF)
+    near = remote(doc_send, doc_near, near_ss, near_rs, sibling)
+    near.start()
+
+    for n in range(2, 5):
+        small_load(n).wait()
+
+    def normed(rows):
+        centre = jnp.mean(rows, axis=1, keepdims=True)
+        spread = jnp.mean(jnp.square(rows - centre), axis=1, keepdims=True)
+        return ((rows - centre) * lax.rsqrt(spread + 1e-05) * gain_ref[...] + bias_ref[...]).astype(BF)
+
+    late_load(2).wait()
+    def documents():
+        drain(doc_recv, doc_rs)
+        pieces = [doc_recv[h].astype(F32) for h in range(CHIPS)]
+        opened = jnp.concatenate(
+            [
+                jnp.where(low, pieces[2 * j], pltpu.roll(pieces[2 * j + 1], 64, 1))
+                for j in range(CHIPS // 2)
+            ],
+            axis=1,
+        )
+        y = jnp.dot(opened.astype(BF), wo[...], preferred_element_type=F32)
+        doc_ref[...] = jnp.tanh(
+            jnp.dot(normed(opened[8:] + y[:8]), wp[...], preferred_element_type=F32)
+            + pbias_ref[...]
+        )
+
 
     late_load(1).wait()
     for g in range(4):
+        if g == 3:
+            documents()
         drain(att_recv.at[pl.ds(0, 4)], att_rs.at[g])
         x = ahead_x[g]
         for p in range(2):
@@ -355,54 +383,31 @@
             s = slice(128 * p, 128 * p + 128)
             lhs[0:128, s] = top.astype(BF)
             lhs[128:256, s] = bottom.astype(BF)
-        if g == 3:
-            drain(doc_recv, doc_rs)
         heads = pl.ds(pl.multiple_of(x * 256, 256), 256)
         y = jnp.dot(lhs[...], wo[heads, :], preferred_element_type=F32)
         if g == 0:
             mixed[...] = tok_ref[...].astype(F32) + y
         else:
             mixed[...] = mixed[...] + y
-
-    pieces = [
-        doc_recv[2 * h].astype(F32) + doc_recv[2 * h + 1].astype(F32) for h in range(CHIPS)
-    ]
-    opened = jnp.concatenate(
-        [
-            jnp.where(low, pieces[2 * j], pltpu.roll(pieces[2 * j + 1], 64, 1))
-            for j in range(CHIPS // 2)
-        ],
-        axis=1,
-    )
-    y = jnp.dot(opened.astype(BF), wo[...], preferred_element_type=F32)
-    opened_mixed = opened[8:] + y[:8]
-
-    def normed(rows):
-        centre = jnp.mean(rows, axis=1, keepdims=True)
-        spread = jnp.mean(jnp.square(rows - centre), axis=1, keepdims=True)
-        return ((rows - centre) * lax.rsqrt(spread + 1e-05) * gain_ref[...] + bias_ref[...]).astype(BF)
-
-    for n in range(2, 5):
-        small_load(n).wait()
-
-    def norm_step(n, carry):
-        rows = pl.ds(pl.multiple_of(n * 64, 64), 64)
+        if g == 0:
+            near.wait_recv()
+            doc_sum[...] = (doc_send[...].astype(F32) + doc_near[...].astype(F32)).astype(BF)
+            for k in others:
+                doc_copy(k).start()
+            pltpu.make_async_copy(doc_sum, doc_recv.at[chip], doc_rs).start()
+
+    for n in range(8):
+        rows = slice(32 * n, 32 * n + 32)
         enc_ref[rows, :] = normed(mixed[rows, :])
-        return carry
-
-    lax.fori_loop(0, 4, norm_step, 0)
-    late_load(2).wait()
-    doc_ref[...] = jnp.tanh(
-        jnp.dot(normed(opened_mixed), wp[...], preferred_element_type=F32) + pbias_ref[...]
-    )
-
-    others = pl.ds(0, CHIPS - 1)
-    drain(ids_recv.at[others], ids_ss)
-    drain(kv_send.at[others], kv_ss)
-    drain(q_send.at[others], q_ss)
-    drain(att_send.at[others], att_ss)
+
+    most = pl.ds(0, CHIPS - 1)
+    drain(ids_recv.at[most], ids_ss)
+    drain(kv_send.at[most], kv_ss)
+    drain(q_send.at[most], q_ss)
+    drain(att_send.at[most], att_ss)
     drain(kv_send, sib_ss)
-    drain(doc_recv.at[pl.ds(0, SHARDS - 1)], doc_ss)
+    near.wait_send()
+    drain(doc_recv.at[most], doc_ss)
 
 
 def per_device(
@@ -433,10 +438,11 @@
             pltpu.VMEM((CHIPS, QROWS, 128), BF),
             pltpu.VMEM((CHIPS, 8, 16, 128), BF),
             pltpu.VMEM((CHIPS, 8, 16, 128), BF),
-            pltpu.VMEM((16, 128), BF),
-            pltpu.VMEM((SHARDS, 16, 128), BF),
-            pltpu.VMEM((CHIPS, RAND, 4, HEADS), jnp.int32),
-            pltpu.SMEM((CHIPS, RAND, 4, HEADS), jnp.int32),
+            pltpu.VMEM((16, 128), BF), pltpu.VMEM((16, 128), BF), pltpu.VMEM((16, 128), BF),
+            pltpu.VMEM((CHIPS, 16, 128), BF),
+            pltpu.VMEM((1, 256), jnp.int32),
+            pltpu.VMEM((CHIPS, 1, 256), jnp.int32),
+            pltpu.SMEM((CHIPS, 1, 256), jnp.int32),
             pltpu.VMEM((CHIPS * 4, BLK, 256), jnp.int32),
             pltpu.VMEM((4 * STEP, BLK, KEYS), F32),
             pltpu.VMEM((4 * STEP, BLK, KEYS), BF),
@@ -444,7 +450,7 @@
             pltpu.VMEM((ROWS, 256), BF),
             pltpu.VMEM((ROWS, D), F32),
             dma((11,)), dma((9,)), dma, dma, dma, dma((CHIPS,)), dma, dma,
-            dma, dma((GROUPS,)), dma, dma((GROUPS,)), dma, dma,
+            dma, dma((GROUPS,)), dma, dma((GROUPS,)), dma, dma, dma, dma,
         ],
         compiler_params=pltpu.CompilerParams(
             collective_id=0, has_side_effects=True, vmem_limit_bytes=32 << 20

time: 46.7 us -> 45.9 us (0.983)
  Pallas kernels: 44.5 us -> 43.7 us
    pallas_call x1, Pallas kernels: 44.5 us -> 43.7 us  [per_device(): pl.pallas_call(kernel, out_shape=(jax.ShapeDtypeStruct((ROWS, D), BF), ja...]
where the time goes in v4:
time: 45.9 us; the launch traced here: 45.8 us
  Pallas kernels  43.7 us (95%)
  local copies, waits for them, and re-layouts  1.41 us (3%)
  between operations  0.64 us (1%)
    pallas_call x1, Pallas kernels, per_device(): pl.pallas_call(kernel, out_shape=(jax.ShapeDtypeStruct((ROWS, D), BF), ja...  43.7 us
    unnamed x2, local copies, waits for them, and re-layouts  1.41 us

profile of v4, /device:TPU:1, one launch (start us, length us, event | category | flops | bytes accessed | tf_op | source)
XLA Modules:
  0.0 45.8 jit_solution(12850341200127680597)
XLA Ops:
  0.6 43.7 %shard_map.122 = (bf16[256,1024]{1,0:T(8,128)(2,1)S(1)}, f32[8,1024]{1,0:T(8,128)S(1)}) custom-call(s32[3,4,16]{2,1,0:T(4,128)} %bitcast.4, s32[8]{0:T(128)} %len_hbm.1, bf16[256,1024]{1,0:T(8,128)(2,1)} %tok_hbm.1, f32[1,1024]{1,0:T(1,128)} %bitcast.5, f32[1,1024]{1,0:T(1,128)} %bitcast.6, f32[1,1024]{1,0:T(1,128)} %bitcast.7, bf16[1024,1024]{1,0:T(8,128)(2,1)} %wq_hbm.1, ...), custom_call_target="tpu_custom_call" | custom-call | tf_op jit(solution)/shard_map/pallas_call | solution.py:421
  44.3 0.8 %copy.15 = bf16[256,1024]{1,0:T(8,128)(2,1)} copy(bf16[256,1024]{1,0:T(8,128)(2,1)S(1)} %get-tuple-element.4) | data formatting | bytes 1048576
  45.1 0.6 %copy.16 = f32[8,1024]{1,0:T(8,128)} copy(f32[8,1024]{1,0:T(8,128)S(1)} %get-tuple-element.5) | data formatting | bytes 65536

commit v5 on v4

--- a/solution.py
+++ b/solution.py
@@ -29,6 +29,11 @@
 ORDER_X = (3, 2, 1, 0)
 ORDER_Z = (0, 1, 3, 2)
 OWN = 12
+KV_STEPS = (
+    (1, 0), (3, 0), (0, 2), (1, 2), (3, 2), (0, 1), (0, 3), (1, 1),
+    (3, 3), (2, 2), (1, 3), (3, 1), (2, 0), (2, 1), (2, 3),
+)
+KV_ORDER = [SIDE * ORDER_X.index(dx) + ORDER_Z.index(dz) for dx, dz in KV_STEPS]
 STEP = 4
 GROUPS = CHIPS // STEP
 
@@ -167,7 +172,7 @@
 
     for k in others:
         ids_copy(k).start()
-    for k in others:
+    for k in KV_ORDER:
         kv_copy(k).start()
     pltpu.make_async_copy(ids_row, ids_recv.at[chip], ids_rs).start()
     sib_copy(OWN).start()
@@ -234,7 +239,7 @@
     to_smem = pltpu.make_async_copy(ids_recv, ids_smem, own_sem.at[3])
     to_smem.start()
     make_masks(OWN)
-    for k in others:
+    for k in KV_ORDER:
         make_masks(k)
         kv_copy(k).wait_recv()
         sib_copy(k).start()

time: 45.9 us -> 44.6 us (0.972)
  Pallas kernels: 43.7 us -> 42.4 us
    pallas_call x1, Pallas kernels: 43.7 us -> 42.4 us  [per_device(): pl.pallas_call(kernel, out_shape=(jax.ShapeDtypeStruct((ROWS, D), BF), ja...]
where the time goes in v5:
time: 44.6 us; the launch traced here: 44.5 us
  Pallas kernels  42.4 us (95%)
  local copies, waits for them, and re-layouts  1.41 us (3%)
  between operations  0.64 us (1%)
    pallas_call x1, Pallas kernels, per_device(): pl.pallas_call(kernel, out_shape=(jax.ShapeDtypeStruct((ROWS, D), BF), ja...  42.4 us
    unnamed x2, local copies, waits for them, and re-layouts  1.41 us

profile of v5, /device:TPU:1, one launch (start us, length us, event | category | flops | bytes accessed | tf_op | source)
XLA Modules:
  0.0 44.5 jit_solution(12722459758691565635)
XLA Ops:
  0.6 42.4 %shard_map.122 = (bf16[256,1024]{1,0:T(8,128)(2,1)S(1)}, f32[8,1024]{1,0:T(8,128)S(1)}) custom-call(s32[3,4,16]{2,1,0:T(4,128)} %bitcast.4, s32[8]{0:T(128)} %len_hbm.1, bf16[256,1024]{1,0:T(8,128)(2,1)} %tok_hbm.1, f32[1,1024]{1,0:T(1,128)} %bitcast.5, f32[1,1024]{1,0:T(1,128)} %bitcast.6, f32[1,1024]{1,0:T(1,128)} %bitcast.7, bf16[1024,1024]{1,0:T(8,128)(2,1)} %wq_hbm.1, ...), custom_call_target="tpu_custom_call" | custom-call | tf_op jit(solution)/shard_map/pallas_call | solution.py:426
  43.1 0.8 %copy.15 = bf16[256,1024]{1,0:T(8,128)(2,1)} copy(bf16[256,1024]{1,0:T(8,128)(2,1)S(1)} %get-tuple-element.4) | data formatting | bytes 1048576
  43.9 0.6 %copy.16 = f32[8,1024]{1,0:T(8,128)} copy(f32[8,1024]{1,0:T(8,128)S(1)} %get-tuple-element.5) | data formatting | bytes 65536

commit v6 on v5

--- a/solution.py
+++ b/solution.py
@@ -33,6 +33,7 @@
     (1, 0), (3, 0), (0, 2), (1, 2), (3, 2), (0, 1), (0, 3), (1, 1),
     (3, 3), (2, 2), (1, 3), (3, 1), (2, 0), (2, 1), (2, 3),
 )
+Q_ORDER = (0, 8, 1, 9, 2, 10, 3, 11, 4, 5, 6, 7, 13, 14, 15)
 KV_ORDER = [SIDE * ORDER_X.index(dx) + ORDER_Z.index(dz) for dx, dz in KV_STEPS]
 STEP = 4
 GROUPS = CHIPS // STEP
@@ -210,7 +211,7 @@
         return carry
 
     lax.fori_loop(0, 4, q_step, 0)
-    for k in others:
+    for k in Q_ORDER:
         q_copy(k).start()
     pltpu.make_async_copy(q_send.at[chip], q_recv.at[OWN], q_rs.at[OWN // STEP]).start()
 

time: 44.6 us -> 44.3 us (level)
  no operation moved by 1% of the time
where the time goes in v6:
time: 44.3 us; the launch traced here: 44.2 us
  Pallas kernels  42.2 us (95%)
  local copies, waits for them, and re-layouts  1.41 us (3%)
  between operations  0.64 us (1%)
    pallas_call x1, Pallas kernels, per_device(): pl.pallas_call(kernel, out_shape=(jax.ShapeDtypeStruct((ROWS, D), BF), ja...  42.2 us
    unnamed x2, local copies, waits for them, and re-layouts  1.41 us

profile of v6, /device:TPU:1, one launch (start us, length us, event | category | flops | bytes accessed | tf_op | source)
XLA Modules:
  0.0 44.2 jit_solution(9747516212307627767)
XLA Ops:
  0.6 42.2 %shard_map.122 = (bf16[256,1024]{1,0:T(8,128)(2,1)S(1)}, f32[8,1024]{1,0:T(8,128)S(1)}) custom-call(s32[3,4,16]{2,1,0:T(4,128)} %bitcast.4, s32[8]{0:T(128)} %len_hbm.1, bf16[256,1024]{1,0:T(8,128)(2,1)} %tok_hbm.1, f32[1,1024]{1,0:T(1,128)} %bitcast.5, f32[1,1024]{1,0:T(1,128)} %bitcast.6, f32[1,1024]{1,0:T(1,128)} %bitcast.7, bf16[1024,1024]{1,0:T(8,128)(2,1)} %wq_hbm.1, ...), custom_call_target="tpu_custom_call" | custom-call | tf_op jit(solution)/shard_map/pallas_call | solution.py:427
  42.8 0.8 %copy.15 = bf16[256,1024]{1,0:T(8,128)(2,1)} copy(bf16[256,1024]{1,0:T(8,128)(2,1)S(1)} %get-tuple-element.4) | data formatting | bytes 1048576
  43.6 0.6 %copy.16 = f32[8,1024]{1,0:T(8,128)} copy(f32[8,1024]{1,0:T(8,128)S(1)} %get-tuple-element.5) | data formatting | bytes 65536
